TPU v7x, 32 devices: a whole 2x2x4 slice. The times are simulated.
32 devices in a mesh: aux: 4 (over x, core), row: 8 (over z, y).
Axes of the slice: x: 2, y: 2, z: 4, core: 2. Of those that a mesh axis runs over, the one named last changes fastest.
Arguments:
- integrals: bfloat16 [4, 8192, 8192], P('aux', 'row'), may hold values from -6 to 6
- orbitals: bfloat16 [8192, 768], P('row'), may hold values from -0.0011901855 to 0.0011901855
Outputs:
- exchange_matrix: float32 [8192, 8192], P('row', 'aux')
All inputs are finite; a program needn't handle non-finite values.
Results may differ from a plain program's by a relative error of at most 0.0033.
Values may be sent and summed in bfloat16 or wider, within the bound.
A program may use at most 128 MiB of HBM per device.

v0:
```python
import jax
import jax.numpy as jnp
from jax import lax
from jax.sharding import PartitionSpec as P


def gather_orbitals(orbitals):
    rows = orbitals.shape[0] // lax.axis_size("aux")
    share = lax.dynamic_slice_in_dim(orbitals, lax.axis_index("aux") * rows, rows, axis=0)
    return lax.all_gather(share, ("row", "aux"), axis=0, tiled=True)


def column_halves(own_half):
    aux, row = lax.axis_size("aux"), lax.axis_size("row")
    span = row // aux
    moves = [
        (p * row + r, (r // span) * row + p * span + r % span)
        for p in range(aux)
        for r in range(row)
    ]
    moved = lax.ppermute(own_half, ("aux", "row"), moves)
    gathered = lax.all_gather(moved, "row", axis=0, tiled=False)
    parts = gathered.reshape((aux, span) + own_half.shape)
    parts = jnp.moveaxis(parts, 2, 1)
    return parts.reshape(aux * own_half.shape[0], span * own_half.shape[1], own_half.shape[2])


def body(integrals, orbitals):
    transformed = jnp.einsum(
        "arn,no->aro",
        integrals,
        gather_orbitals(orbitals),
        preferred_element_type=jnp.float32,
    )
    own_half = transformed.astype(jnp.bfloat16)
    columns = column_halves(own_half)
    rows = lax.all_gather(own_half, "aux", axis=0, tiled=True)
    return jnp.einsum("aro,aco->rc", rows, columns, preferred_element_type=jnp.float32)


def solution(mesh):
    in_specs = (P("aux", "row", None), P("row", None))
    out_specs = P("row", "aux")
    return jax.shard_map(body, mesh=mesh, in_specs=in_specs, out_specs=out_specs, check_vma=False)
```

profile of v0, /device:TPU:2, one launch (start us, length us, event | category | flops | bytes accessed | tf_op | source)
XLA Modules:
  0.0 406.7 jit_solution(16350279765923195468)
XLA Ops:
  6.5 0.0 copy-start
  6.5 0.0 all-gather.6.cloned.1.call-start
  6.5 1.4 copy-done
  7.9 0.8 constant_dynamic-slice_fusion
  8.7 0.0 all-gather.6.cloned.1.call-update
  8.7 0.0 all-gather.8.cloned.1.call-start
  8.8 97.8 %all-gather.6.cloned.1.call-done = bf16[8192,768]{1,0:T(8,128)(2,1)} async-done(((bf16[256,768]{1,0:T(8,128)(2,1)}), bf16[8192,768]{1,0:T(8,128)(2,1)}) %all-gather.6.cloned.1.call-update) | async-done | bytes 12582928 | tf_op jit(solution)/shard_map/all_gather | solution.py:10
  106.6 20.0 %fusion.2 = bf16[768,1024]{1,0:T(8,128)(2,1)} fusion(bf16[8192,768]{1,0:T(8,128)(2,1)} %all-gather.6.cloned.1.call-done, bf16[1,1024,8192]{2,1,0:T(8,128)(2,1)} %param.2), kind=kOutput, calls=%fused_computation.3 | convolution fusion | flops 12885688320 | bytes 30932992 | tf_op jit(solution)/shard_map/arn,no->aro/dot_general | solution.py:29
  126.6 0.0 all-gather.8.cloned.1.call-update
  126.6 0.0 all-gather.10.cloned.1.call-start
  126.6 3.8 collective-permute-start
  130.4 70.3 %collective-permute-done = bf16[1,1024,768]{1,2,0:T(8,128)(2,1)S(1)} collective-permute-done((bf16[1,1024,768]{1,2,0:T(8,128)(2,1)}, bf16[1,1024,768]{1,2,0:T(8,128)(2,1)S(1)}, u32[]{:S(2)}, u32[]{:S(2)}) %collective-permute-start) | collective-permute-done | bytes 1572896 | tf_op jit(solution)/shard_map/ppermute | solution.py:21
  200.7 1.6 copy.6
  202.3 0.0 all-gather.10.cloned.1.call-update
  202.3 1.8 all-gather.8.cloned.1.call-done
  204.2 8.7 %copy.8 = bf16[4096,768]{1,0:T(8,128)(2,1)} copy(bf16[4096,768]{0,1:T(8,128)(2,1)} %all-gather.8.cloned.1.call-done) | data formatting | bytes 12582912 | tf_op jit(solution)/shard_map/all_gather | solution.py:37
  212.9 168.3 %all-gather.10.cloned.1.call-done = bf16[8,1024,768]{2,1,0:T(8,128)(2,1)} async-done(((bf16[1,1024,768]{2,1,0:T(8,128)(2,1)}), bf16[8,1024,768]{2,1,0:T(8,128)(2,1)}) %all-gather.10.cloned.1.call-update) | async-done | bytes 12582928 | tf_op jit(solution)/shard_map/all_gather | solution.py:22
  381.2 0.0 copy-start.1
  381.2 19.0 %convolution_bitcast_fusion = f32[1024,2048]{1,0:T(8,128)} fusion(bf16[4,1024,768]{2,1,0:T(8,128)(2,1)} %bitcast.15, bf16[4,2048,768]{2,1,0:T(8,128)(2,1)} %bitcast.18), kind=kOutput, calls=%fused_computation.2 | convolution fusion | flops 12884901888 | bytes 27262976 | tf_op jit(solution)/shard_map/aro,aco->rc/dot_general | solution.py:38
  400.2 0.0 copy-done.1
Async XLA Ops:
  6.5 1.4 copy-start
  6.5 100.0 %all-gather.6.cloned.1.call-start = ((), (), s32[]{:S(2)}) async-start(), calls=%async_computation | async-start | bytes 12976128 | tf_op jit(solution)/shard_map/all_gather | solution.py:10
  8.7 195.4 %all-gather.8.cloned.1.call-start = ((), (), s32[]{:S(2)}) async-start(), calls=%async_computation.1 | async-start | bytes 7864320 | tf_op jit(solution)/shard_map/all_gather | solution.py:37
  126.6 254.6 %all-gather.10.cloned.1.call-start = ((), (), s32[]{:S(2)}) async-start(), calls=%async_computation.2 | async-start | bytes 14155776 | tf_op jit(solution)/shard_map/all_gather | solution.py:22
  126.6 74.1 %collective-permute-start = (bf16[1,1024,768]{1,2,0:T(8,128)(2,1)}, bf16[1,1024,768]{1,2,0:T(8,128)(2,1)S(1)}, u32[]{:S(2)}, u32[]{:S(2)}) collective-permute-start(bf16[1,1024,768]{1,2,0:T(8,128)(2,1)} %bitcast.17), channel_id=1, source_target_pairs={{0,0},{1,1},{2,8},{3,9},{4,16},{5,17},{6,24},{7,25},{8,2},{9,3},{1... | collective-permute-start | bytes 4718600 | tf_op jit(solution)/shard_map/ppermute | solution.py:21
  381.2 19.0 %copy-start.1 = (bf16[1024,768]{1,0:T(8,128)(2,1)S(1)}, bf16[1024,768]{1,0:T(8,128)(2,1)}, u32[]{:S(2)}) copy-start(bf16[1024,768]{1,0:T(8,128)(2,1)} %param.3) | copy-start | bytes 4718596
Sparse Core Ops, SparseCore 0:
  10.2 96.3 all-gather.5
  126.7 77.4 all-gather.7
  206.4 174.7 all-gather.9
where the time goes:
time: 409 us; the launch traced here: 407 us
  waiting for transfers between devices  338 us (83%)
  matrix products  38.9 us (10%)
  between operations  13.1 us (3%)
  local copies, waits for them, and re-layouts  12.5 us (3%)
    all_gather x1, waiting for transfers between devices, column_halves(): gathered = lax.all_gather(moved, 'row', axis=0, tiled=False)  168 us
    all_gather x1, waiting for transfers between devices, gather_orbitals(): return lax.all_gather(share, ('row', 'aux'), axis=0, tiled=True)  97.8 us
    ppermute x1, waiting for transfers between devices, column_halves(): moved = lax.ppermute(own_half, ('aux', 'row'), moves)  70.3 us
    dot_general x1, matrix products, body(): jnp.einsum('arn,no->aro', integrals, gather_orbitals(orbitals), preferred...  20 us
    dot_general x1, matrix products, body(): jnp.einsum('aro,aco->rc', rows, columns, preferred_element_type=jnp.float32)  19 us
    all_gather x1, local copies, waits for them, and re-layouts, body(): rows = lax.all_gather(own_half, 'aux', axis=0, tiled=True)  8.71 us
  transfers between devices with their start and end apart: 4, of which 4 were waited for; matrix products, arithmetic and copies ran while one was open for 3% of the time, Pallas kernels for 0%

commit v1 on v0

v1 whole, which is shorter than its diff:
```python
import functools

import jax
import jax.numpy as jnp
from jax import lax
from jax.experimental import pallas as pl
from jax.experimental.pallas import tpu as pltpu
from jax.sharding import PartitionSpec as P

MESH = pl.DeviceIdType.MESH
CHUNK = 128
TILE = 256


def kernel(aux, rows_axis, b_hbm, c_hbm, out_hbm, b, c, h, k_acc, h_acc, *sems):
    (local_b, local_c, cz_s, cz_r, cy_s, cy_r, cx_s, cx_r,
     hx_s, hx_r, hz_s, hz_r, hy_s, hy_r, out_sem) = sems
    span = rows_axis // aux
    chunks, _, n_rows, width = c.shape
    share = n_rows // aux
    p = lax.axis_index("aux")
    r = lax.axis_index("row")
    layer = lax.div(r, span)
    member = lax.rem(r, span)
    bits = []
    bit = aux // 2
    while bit:
        bits.append(bit)
        bit //= 2

    def row_of(at_layer, at_member):
        return at_layer * span + at_member

    next_member = row_of(layer, lax.rem(member + 1, span))
    last_member = row_of(layer, lax.rem(member + span - 1, span))
    owner = layer == p
    own_slot = jnp.where(owner, 0, 1 + member)

    def to_row(row):
        return {"device_id": {"row": row}, "device_id_type": MESH}

    def to_aux(index):
        return {"device_id": {"aux": index}, "device_id_type": MESH}

    def lower(k):
        low = k & -k if k else aux
        return [bit for bit in bits if bit < low]

    def c_piece(j, row):
        return c.at[j, row, pl.ds(pl.multiple_of(p * share, share), share)]

    def c_line(j, at_layer, way):
        piece = c_piece(j, row_of(at_layer, member))
        return pltpu.make_async_remote_copy(
            piece, piece, cz_s.at[way, j, at_layer], cz_r.at[j, at_layer],
            **to_row(row_of(layer + 2 * way - 1, member)))

    def c_member(j, at_layer, step):
        line = lax.rem(member + span - step, span)
        piece = c_piece(j, row_of(at_layer, line))
        return pltpu.make_async_remote_copy(
            piece, piece, cy_s.at[j, step, at_layer], cy_r.at[j, step, at_layer], **to_row(next_member))

    def c_aux(j, k, bit):
        source = jnp.bitwise_xor(p, k)
        piece = c.at[j, :, pl.ds(pl.multiple_of(source * share, share), share)]
        return pltpu.make_async_remote_copy(
            piece, piece, cx_s.at[j, k ^ bit], cx_r.at[j, k ^ bit], **to_aux(jnp.bitwise_xor(p, bit)))

    def lanes(k):
        return pl.ds(k * width, width)

    def h_aux(j, k, bit):
        return pltpu.make_async_remote_copy(
            h.at[0, j, :, lanes(k)], h.at[0, j, :, lanes(k ^ bit)], hx_s.at[j, k ^ bit], hx_r.at[j, k ^ bit],
            **to_aux(jnp.bitwise_xor(p, bit)))

    def h_line(j, k, way):
        return pltpu.make_async_remote_copy(
            h.at[own_slot, j, :, lanes(k)], h.at[1 + member, j, :, lanes(k)], hz_s.at[way, j, k], hz_r.at[j, k],
            **to_row(row_of(layer + 2 * way - 1, member)))

    def h_member(j, k, step):
        line = lax.rem(member + span - step, span)
        slot = own_slot if step == 0 else 1 + line
        return pltpu.make_async_remote_copy(
            h.at[slot, j, :, lanes(k)], h.at[1 + line, j, :, lanes(k)], hy_s.at[j, step, k], hy_r.at[j, step, k],
            **to_row(next_member))

    up, down = layer + 1 < aux, layer > 0

    barrier = pltpu.get_barrier_semaphore()
    for bit in bits:
        pl.semaphore_signal(barrier, 1, **to_aux(jnp.bitwise_xor(p, bit)))
    pl.semaphore_signal(barrier, 1, **to_row(next_member))
    pl.semaphore_signal(barrier, 1, **to_row(last_member))

    @pl.when(up)
    def _():
        pl.semaphore_signal(barrier, 1, **to_row(row_of(layer + 1, member)))

    @pl.when(down)
    def _():
        pl.semaphore_signal(barrier, 1, **to_row(row_of(layer - 1, member)))

    def own_c(j):
        return pltpu.make_async_copy(
            c_hbm.at[pl.ds(pl.multiple_of(p * share, share), share), pl.ds(pl.multiple_of(j * width, width), width)],
            c_piece(j, r), local_c.at[j])

    for j in range(chunks):
        own_c(j).start()
    load_b = pltpu.make_async_copy(b_hbm, b, local_b)
    load_b.start()
    pl.semaphore_wait(barrier, len(bits) + 2 + up.astype(jnp.int32) + down.astype(jnp.int32))

    def loop(count, body):
        def step(i, carry):
            body(i)
            return carry
        lax.fori_loop(0, count, step, 0)

    def pass_c(j, at_layer):
        c_member(j, at_layer, 0).start()

    def start_c(j):
        own_c(j).wait()

        @pl.when(up)
        def _():
            c_line(j, layer, 1).start()

        @pl.when(down)
        def _():
            c_line(j, layer, 0).start()

        pass_c(j, layer)

    def relay_c(j):
        for step in range(1, aux):
            @pl.when(layer - step >= 0)
            def _():
                c_line(j, layer - step, 1).wait_recv()

                @pl.when(up)
                def _():
                    c_line(j, layer - step, 1).start()

                pass_c(j, layer - step)

            @pl.when(layer + step < aux)
            def _():
                c_line(j, layer + step, 0).wait_recv()

                @pl.when(down)
                def _():
                    c_line(j, layer + step, 0).start()

                pass_c(j, layer + step)

    def spread_c(j):
        for step in range(span - 1):
            for at_layer in range(aux):
                c_member(j, at_layer, step).wait_recv()
                if step + 1 < span - 1:
                    c_member(j, at_layer, step + 1).start()
        for bit in bits:
            c_aux(j, 0, bit).start()

    def finish_c(j):
        for k in sorted(range(1, aux), key=lambda k: -(k & -k)):
            c_aux(j, k ^ (k & -k), k & -k).wait_recv()
            for bit in lower(k):
                c_aux(j, k, bit).start()

    def transform(j):
        finish_c(j)

        def block(i):
            part = jnp.dot(
                b[:, pl.ds(pl.multiple_of(i * n_rows, n_rows), n_rows)], c[j, i], preferred_element_type=jnp.float32)

            @pl.when(i == 0)
            def _():
                h_acc[...] = part

            @pl.when(i > 0)
            def _():
                h_acc[...] += part

        loop(rows_axis, block)
        h[0, j, :, lanes(0)] = h_acc[...].astype(h.dtype)
        for bit in bits:
            h_aux(j, 0, bit).start()

    def send_h(j, k):
        @pl.when(owner)
        def _():
            @pl.when(up)
            def _():
                h_line(j, k, 1).start()

            @pl.when(down)
            def _():
                h_line(j, k, 0).start()

            h_member(j, k, 0).start()

    def take_h(j, k):
        h_aux(j, k ^ (k & -k), k & -k).wait_recv()
        for bit in lower(k):
            h_aux(j, k, bit).start()
        send_h(j, k)

    def send_first(j):
        send_h(j, 0)
        for k in range(1, aux // 2):
            take_h(j, k)

    def send_rest(j):
        for k in range(aux // 2, aux):
            take_h(j, k)

    def relay_h(j, k):
        @pl.when(layer > p)
        def _():
            h_line(j, k, 1).wait_recv()

            @pl.when(up)
            def _():
                h_line(j, k, 1).start()

            h_member(j, k, 0).start()

        @pl.when(layer < p)
        def _():
            h_line(j, k, 0).wait_recv()

            @pl.when(down)
            def _():
                h_line(j, k, 0).start()

            h_member(j, k, 0).start()

    tile = min(TILE, n_rows)
    tiles = n_rows // tile

    def out_copy(n):
        columns = pl.ds(pl.multiple_of(n * tile, tile), tile)
        return pltpu.make_async_copy(k_acc.at[:, columns], out_hbm.at[:, columns], out_sem.at[n])

    def update(j, is_last):
        for step in range(span - 1):
            for k in range(aux):
                h_member(j, k, step).wait_recv()
                if step + 1 < span - 1:
                    h_member(j, k, step + 1).start()

        def block(n):
            line = lax.div(n, tiles)
            slot = jnp.where(line == member, own_slot, 1 + line)
            at = pl.ds(pl.multiple_of(lax.rem(n, tiles) * tile, tile), tile)
            part = lax.dot_general(
                h[0, j], h[slot, j, at], (((1,), (1,)), ((), ())), preferred_element_type=jnp.float32)
            columns = pl.ds(pl.multiple_of(n * tile, tile), tile)
            k_acc[:, columns] += part
            if is_last:
                out_copy(n).start()

        loop(span * tiles, block)

    loop(chunks, start_c)

    def clear(n):
        columns = pl.ds(pl.multiple_of(n * tile, tile), tile)
        k_acc[:, columns] = jnp.zeros((n_rows, tile), jnp.float32)

    loop(span * tiles, clear)

    relay_c(0)
    relay_c(1)
    spread_c(0)
    relay_c(2)
    spread_c(1)
    loop(chunks - 3, lambda i: relay_c(i + 3))
    load_b.wait()
    transform(0)
    send_first(0)
    spread_c(2)
    transform(1)
    send_rest(0)
    send_first(1)
    spread_c(3)

    def main(j):
        half = aux // 2
        for k in range(half):
            relay_h(j, k)

        @pl.when(j + 2 < chunks)
        def _():
            transform(j + 2)

        @pl.when(j + 1 < chunks)
        def _():
            send_rest(j + 1)

        @pl.when(j + 2 < chunks)
        def _():
            send_first(j + 2)

        @pl.when(j + 4 < chunks)
        def _():
            spread_c(j + 4)

        for k in range(half, aux):
            relay_h(j, k)

        @pl.when(j > 0)
        def _():
            update(j - 1, False)

    loop(chunks, main)
    update(chunks - 1, True)

    def drain(j):
        for at_layer in range(aux):
            @pl.when(jnp.logical_and(up, at_layer <= layer))
            def _():
                c_line(j, at_layer, 1).wait_send()

            @pl.when(jnp.logical_and(down, at_layer >= layer))
            def _():
                c_line(j, at_layer, 0).wait_send()

            for step in range(span - 1):
                c_member(j, at_layer, step).wait_send()
        for k in range(1, aux):
            low = k & -k
            c_aux(j, k ^ low, low).wait_send()
            h_aux(j, k ^ low, low).wait_send()
        for k in range(aux):
            @pl.when(jnp.logical_and(up, layer >= p))
            def _():
                h_line(j, k, 1).wait_send()

            @pl.when(jnp.logical_and(down, layer <= p))
            def _():
                h_line(j, k, 0).wait_send()

            for step in range(span - 1):
                h_member(j, k, step).wait_send()

    loop(chunks, drain)
    loop(span * tiles, lambda n: out_copy(n).wait())


def body(aux, rows_axis, integrals, orbitals):
    _, n_rows, n = integrals.shape
    occ = orbitals.shape[1]
    span = rows_axis // aux
    width = CHUNK
    chunks = occ // width
    dma = pltpu.SemaphoreType.DMA
    tiles = span * (n_rows // min(TILE, n_rows))
    steps = max(span - 1, 1)
    return pl.pallas_call(
        functools.partial(kernel, aux, rows_axis),
        out_shape=jax.ShapeDtypeStruct((n_rows, span * n_rows), jnp.float32),
        in_specs=[pl.BlockSpec(memory_space=pl.ANY)] * 2,
        out_specs=pl.BlockSpec(memory_space=pl.ANY),
        scratch_shapes=[
            pltpu.VMEM((n_rows, n), integrals.dtype),
            pltpu.VMEM((chunks, rows_axis, n_rows, width), orbitals.dtype),
            pltpu.VMEM((1 + span, chunks, n_rows, aux * width), jnp.bfloat16),
            pltpu.VMEM((n_rows, span * n_rows), jnp.float32),
            pltpu.VMEM((n_rows, width), jnp.float32),
            dma, dma((chunks,)),
            dma((2, chunks, aux)), dma((chunks, aux)),
            dma((chunks, steps, aux)), dma((chunks, steps, aux)),
            dma((chunks, aux)), dma((chunks, aux)),
            dma((chunks, aux)), dma((chunks, aux)),
            dma((2, chunks, aux)), dma((chunks, aux)),
            dma((chunks, steps, aux)), dma((chunks, steps, aux)),
            dma((tiles,)),
        ],
        compiler_params=pltpu.CompilerParams(
            collective_id=0, has_side_effects=True, vmem_limit_bytes=67_043_328),
    )(integrals.reshape(n_rows, n), orbitals)


def solution(mesh):
    aux, rows_axis = mesh.shape["aux"], mesh.shape["row"]
    return jax.shard_map(
        functools.partial(body, aux, rows_axis), mesh=mesh,
        in_specs=(P("aux", "row", None), P("row", None)), out_specs=P("row", "aux"), check_vma=False)
```

time: 409 us -> 231 us (0.56)
  waiting for transfers between devices: 338 us -> 0 us
  Pallas kernels: 0 us -> 222 us
  matrix products: 38.9 us -> 0 us
  between operations: 13.1 us -> 0.01 us
  local copies, waits for them, and re-layouts: 12.5 us -> 7.89 us
    all_gather x3 -> x0, waiting for transfers between devices: 268 us -> none  [the longest x1 168 us: column_halves(): gathered = lax.all_gather(moved, 'row', axis=0, tiled=False)]
    pallas_call x0 -> x1, Pallas kernels: none -> 222 us  [body(): pl.pallas_call(functools.partial(kernel, aux, rows_axis), out_shape=jax.S...]
    ppermute x1 -> x0, waiting for transfers between devices: 70.3 us -> none  [column_halves(): moved = lax.ppermute(own_half, ('aux', 'row'), moves)]
    dot_general x2 -> x0, matrix products: 38.9 us -> none  [the longest x1 20 us: body(): jnp.einsum('arn,no->aro', integrals, gather_orbitals(orbitals), preferred...]
    all_gather x1 -> x0, local copies, waits for them, and re-layouts: 8.71 us -> none  [body(): rows = lax.all_gather(own_half, 'aux', axis=0, tiled=True)]
    unnamed x4 -> x1, local copies, waits for them, and re-layouts: 1.41 us -> 7.89 us
  transfers between devices with their start and end apart: 4 -> 0, of which waited for: 4 -> 0; matrix products, arithmetic and copies ran while one was open for 3% -> 0% of each run, Pallas kernels for 0% -> 0%
where the time goes in v1:
time: 231 us; the launch traced here: 230 us
  Pallas kernels  222 us (96%)
  local copies, waits for them, and re-layouts  7.89 us (3%)
    pallas_call x1, Pallas kernels, body(): pl.pallas_call(functools.partial(kernel, aux, rows_axis), out_shape=jax.S...  222 us
    unnamed x1, local copies, waits for them, and re-layouts  7.89 us

profile of v1, /device:TPU:2, one launch (start us, length us, event | category | flops | bytes accessed | tf_op | source)
XLA Modules:
  0.0 229.9 jit_solution(499134698361568899)
XLA Ops:
  0.0 222.0 %shard_map.28 = f32[1024,2048]{1,0:T(8,128)} custom-call(bf16[1024,8192]{1,0:T(8,128)(2,1)} %bitcast.1, bf16[1024,768]{1,0:T(8,128)(2,1)} %c_hbm.1), custom_call_target="tpu_custom_call" | custom-call | tf_op jit(solution)/shard_map/pallas_call | solution.py:367
  222.0 7.9 %copy.4 = f32[1024,2048]{1,0:T(8,128)} copy(f32[1024,2048]{1,0:T(8,128)} %shard_map.28) | data formatting | bytes 16777216

commit v2 on v1

--- a/solution.py
+++ b/solution.py
@@ -10,6 +10,7 @@
 MESH = pl.DeviceIdType.MESH
 CHUNK = 128
 TILE = 256
+PARTS = 4
 
 
 def kernel(aux, rows_axis, b_hbm, c_hbm, out_hbm, b, c, h, k_acc, h_acc, *sems):
@@ -75,17 +76,31 @@
             h.at[0, j, :, lanes(k)], h.at[0, j, :, lanes(k ^ bit)], hx_s.at[j, k ^ bit], hx_r.at[j, k ^ bit],
             **to_aux(jnp.bitwise_xor(p, bit)))
 
-    def h_line(j, k, way):
-        return pltpu.make_async_remote_copy(
-            h.at[own_slot, j, :, lanes(k)], h.at[1 + member, j, :, lanes(k)], hz_s.at[way, j, k], hz_r.at[j, k],
+    part = n_rows // PARTS
+
+    def message(slot, j, i):
+        rows = pl.ds(pl.multiple_of(lax.rem(i, PARTS) * part, part), part)
+        return h.at[slot, j, rows, pl.ds(pl.multiple_of(lax.div(i, PARTS) * width, width), width)]
+
+    def h_line(j, i, way):
+        return pltpu.make_async_remote_copy(
+            message(own_slot, j, i), message(1 + member, j, i), hz_s.at[way, j], hz_r.at[j, i],
             **to_row(row_of(layer + 2 * way - 1, member)))
 
-    def h_member(j, k, step):
+    def h_line_sent(j, way):
+        return pltpu.make_async_remote_copy(
+            h.at[0, j], h.at[0, j], hz_s.at[way, j], hz_r.at[j, 0], **to_row(row_of(layer + 2 * way - 1, member)))
+
+    def h_member(j, i, step):
         line = lax.rem(member + span - step, span)
         slot = own_slot if step == 0 else 1 + line
         return pltpu.make_async_remote_copy(
-            h.at[slot, j, :, lanes(k)], h.at[1 + line, j, :, lanes(k)], hy_s.at[j, step, k], hy_r.at[j, step, k],
+            message(slot, j, i), message(1 + line, j, i), hy_s.at[j, step], hy_r.at[j, step, i],
             **to_row(next_member))
+
+    def h_member_sent(j, step):
+        return pltpu.make_async_remote_copy(
+            h.at[0, j], h.at[0, j], hy_s.at[j, step], hy_r.at[j, step, 0], **to_row(next_member))
 
     up, down = layer + 1 < aux, layer > 0
 
@@ -114,11 +129,14 @@
     load_b.start()
     pl.semaphore_wait(barrier, len(bits) + 2 + up.astype(jnp.int32) + down.astype(jnp.int32))
 
-    def loop(count, body):
+    def loop_from(first, last, body):
         def step(i, carry):
             body(i)
             return carry
-        lax.fori_loop(0, count, step, 0)
+        lax.fori_loop(first, last, step, 0)
+
+    def loop(count, body):
+        loop_from(0, count, body)
 
     def pass_c(j, at_layer):
         c_member(j, at_layer, 0).start()
@@ -173,38 +191,52 @@
             for bit in lower(k):
                 c_aux(j, k, bit).start()
 
-    def transform(j):
-        finish_c(j)
+    slots = aux * PARTS
+    pieces = slots // 2
+
+    def transform(j, piece):
+        @pl.when(piece == 0)
+        def _():
+            finish_c(j)
+            h_acc[...] = jnp.zeros_like(h_acc)
 
         def block(i):
-            part = jnp.dot(
+            h_acc[...] += jnp.dot(
                 b[:, pl.ds(pl.multiple_of(i * n_rows, n_rows), n_rows)], c[j, i], preferred_element_type=jnp.float32)
 
-            @pl.when(i == 0)
-            def _():
-                h_acc[...] = part
-
-            @pl.when(i > 0)
-            def _():
-                h_acc[...] += part
-
-        loop(rows_axis, block)
-        h[0, j, :, lanes(0)] = h_acc[...].astype(h.dtype)
-        for bit in bits:
-            h_aux(j, 0, bit).start()
+        loop_from(lax.div(piece * rows_axis, pieces), lax.div((piece + 1) * rows_axis, pieces), block)
+
+        @pl.when(piece == pieces - 1)
+        def _():
+            h[0, j, :, lanes(0)] = h_acc[...].astype(h.dtype)
+            for bit in bits:
+                h_aux(j, 0, bit).start()
+
+            @pl.when(j > 0)
+            def _():
+                send_rest(j - 1)
+
+            send_first(j)
+
+            @pl.when(j + 2 < chunks)
+            def _():
+                spread_c(j + 2)
 
     def send_h(j, k):
         @pl.when(owner)
         def _():
-            @pl.when(up)
-            def _():
-                h_line(j, k, 1).start()
-
-            @pl.when(down)
-            def _():
-                h_line(j, k, 0).start()
-
-            h_member(j, k, 0).start()
+            def send(i):
+                @pl.when(up)
+                def _():
+                    h_line(j, i, 1).start()
+
+                @pl.when(down)
+                def _():
+                    h_line(j, i, 0).start()
+
+                h_member(j, i, 0).start()
+
+            loop_from(k * PARTS, (k + 1) * PARTS, send)
 
     def take_h(j, k):
         h_aux(j, k ^ (k & -k), k & -k).wait_recv()
@@ -221,53 +253,69 @@
         for k in range(aux // 2, aux):
             take_h(j, k)
 
-    def relay_h(j, k):
+    def relay_h(j, i):
         @pl.when(layer > p)
         def _():
-            h_line(j, k, 1).wait_recv()
+            h_line(j, i, 1).wait_recv()
 
             @pl.when(up)
             def _():
-                h_line(j, k, 1).start()
-
-            h_member(j, k, 0).start()
+                h_line(j, i, 1).start()
+
+            h_member(j, i, 0).start()
 
         @pl.when(layer < p)
         def _():
-            h_line(j, k, 0).wait_recv()
+            h_line(j, i, 0).wait_recv()
 
             @pl.when(down)
             def _():
-                h_line(j, k, 0).start()
-
-            h_member(j, k, 0).start()
+                h_line(j, i, 0).start()
+
+            h_member(j, i, 0).start()
 
     tile = min(TILE, n_rows)
     tiles = n_rows // tile
+    all_tiles = span * tiles
 
     def out_copy(n):
         columns = pl.ds(pl.multiple_of(n * tile, tile), tile)
         return pltpu.make_async_copy(k_acc.at[:, columns], out_hbm.at[:, columns], out_sem.at[n])
 
-    def update(j, is_last):
+    def take_members(j, first, last):
         for step in range(span - 1):
-            for k in range(aux):
-                h_member(j, k, step).wait_recv()
+            def take(i):
+                h_member(j, i, step).wait_recv()
                 if step + 1 < span - 1:
-                    h_member(j, k, step + 1).start()
-
-        def block(n):
-            line = lax.div(n, tiles)
-            slot = jnp.where(line == member, own_slot, 1 + line)
-            at = pl.ds(pl.multiple_of(lax.rem(n, tiles) * tile, tile), tile)
-            part = lax.dot_general(
-                h[0, j], h[slot, j, at], (((1,), (1,)), ((), ())), preferred_element_type=jnp.float32)
-            columns = pl.ds(pl.multiple_of(n * tile, tile), tile)
-            k_acc[:, columns] += part
-            if is_last:
-                out_copy(n).start()
-
-        loop(span * tiles, block)
+                    h_member(j, i, step + 1).start()
+            loop_from(first, last, take)
+
+    def add_tile(j, n, first, last):
+        line = lax.div(n, tiles)
+        slot = jnp.where(line == member, own_slot, 1 + line)
+        at = pl.ds(pl.multiple_of(lax.rem(n, tiles) * tile, tile), tile)
+        some = pl.ds(first * width, (last - first) * width)
+        k_acc[:, pl.ds(pl.multiple_of(n * tile, tile), tile)] += lax.dot_general(
+            h[0, j, :, some], h[slot, j, at, some], (((1,), (1,)), ((), ())), preferred_element_type=jnp.float32)
+
+    def update(j, piece, count):
+        @pl.when(piece == 0)
+        def _():
+            take_members(j, 0, slots)
+
+        loop_from(lax.div(piece * all_tiles, count), lax.div((piece + 1) * all_tiles, count),
+                  lambda n: add_tile(j, n, 0, aux))
+
+    def last_update(j):
+        take_members(j, 0, slots - PARTS)
+        loop(all_tiles, lambda n: add_tile(j, n, 0, aux - 1))
+        take_members(j, slots - PARTS, slots)
+
+        def finish(n):
+            add_tile(j, n, aux - 1, aux)
+            out_copy(n).start()
+
+        loop(all_tiles, finish)
 
     loop(chunks, start_c)
 
@@ -284,44 +332,35 @@
     spread_c(1)
     loop(chunks - 3, lambda i: relay_c(i + 3))
     load_b.wait()
-    transform(0)
-    send_first(0)
-    spread_c(2)
-    transform(1)
-    send_rest(0)
-    send_first(1)
-    spread_c(3)
+    loop(pieces, lambda piece: transform(0, piece))
+
+    quarter = slots // 4
 
     def main(j):
-        half = aux // 2
-        for k in range(half):
-            relay_h(j, k)
-
-        @pl.when(j + 2 < chunks)
-        def _():
-            transform(j + 2)
-
-        @pl.when(j + 1 < chunks)
-        def _():
-            send_rest(j + 1)
-
-        @pl.when(j + 2 < chunks)
-        def _():
-            send_first(j + 2)
-
-        @pl.when(j + 4 < chunks)
-        def _():
-            spread_c(j + 4)
-
-        for k in range(half, aux):
-            relay_h(j, k)
-
-        @pl.when(j > 0)
-        def _():
-            update(j - 1, False)
+        def slot(i):
+            relay_h(j, i)
+            early = jnp.logical_and(j == 1, i < quarter)
+            chunk = jnp.where(j == 0, jnp.where(i < pieces, 1, 2), jnp.where(early, 2, j + 2))
+            piece = jnp.where(
+                j == 0, jnp.where(i < pieces, i, i - 3 * quarter), jnp.where(early, i + quarter, i - quarter))
+            now = jnp.logical_and(jnp.logical_and(piece >= 0, piece < pieces), chunk < chunks)
+
+            @pl.when(now)
+            def _():
+                transform(chunk, piece)
+
+            @pl.when(jnp.logical_and(j > 0, i >= 3 * quarter))
+            def _():
+                update(j - 1, i - 3 * quarter, quarter)
+
+        loop(slots, slot)
+
+        @pl.when(j == max(chunks - 2, 0))
+        def _():
+            send_rest(chunks - 1)
 
     loop(chunks, main)
-    update(chunks - 1, True)
+    last_update(chunks - 1)
 
     def drain(j):
         for at_layer in range(aux):
@@ -339,20 +378,20 @@
             low = k & -k
             c_aux(j, k ^ low, low).wait_send()
             h_aux(j, k ^ low, low).wait_send()
-        for k in range(aux):
-            @pl.when(jnp.logical_and(up, layer >= p))
-            def _():
-                h_line(j, k, 1).wait_send()
-
-            @pl.when(jnp.logical_and(down, layer <= p))
-            def _():
-                h_line(j, k, 0).wait_send()
-
-            for step in range(span - 1):
-                h_member(j, k, step).wait_send()
+
+        @pl.when(jnp.logical_and(up, layer >= p))
+        def _():
+            h_line_sent(j, 1).wait_send()
+
+        @pl.when(jnp.logical_and(down, layer <= p))
+        def _():
+            h_line_sent(j, 0).wait_send()
+
+        for step in range(span - 1):
+            h_member_sent(j, step).wait_send()
 
     loop(chunks, drain)
-    loop(span * tiles, lambda n: out_copy(n).wait())
+    loop(all_tiles, lambda n: out_copy(n).wait())
 
 
 def body(aux, rows_axis, integrals, orbitals):
@@ -380,8 +419,8 @@
             dma((chunks, steps, aux)), dma((chunks, steps, aux)),
             dma((chunks, aux)), dma((chunks, aux)),
             dma((chunks, aux)), dma((chunks, aux)),
-            dma((2, chunks, aux)), dma((chunks, aux)),
-            dma((chunks, steps, aux)), dma((chunks, steps, aux)),
+            dma((2, chunks)), dma((chunks, aux * PARTS)),
+            dma((chunks, steps)), dma((chunks, steps, aux * PARTS)),
             dma((tiles,)),
         ],
         compiler_params=pltpu.CompilerParams(

time: 231 us -> 208 us (0.900)
  Pallas kernels: 222 us -> 200 us
    pallas_call x1, Pallas kernels: 222 us -> 200 us  [body(): pl.pallas_call(functools.partial(kernel, aux, rows_axis), out_shape=jax.S...]
where the time goes in v2:
time: 208 us
  Pallas kernels  200 us (96%)
  local copies, waits for them, and re-layouts  7.89 us (4%)
    pallas_call x1, Pallas kernels, body(): pl.pallas_call(functools.partial(kernel, aux, rows_axis), out_shape=jax.S...  200 us
    unnamed x1, local copies, waits for them, and re-layouts  7.89 us

profile of v2, /device:TPU:2, one launch (start us, length us, event | category | flops | bytes accessed | tf_op | source)
XLA Modules:
  0.0 208.3 jit_solution(10460929144185104375)
XLA Ops:
  0.0 200.4 %shard_map.28 = f32[1024,2048]{1,0:T(8,128)} custom-call(bf16[1024,8192]{1,0:T(8,128)(2,1)} %bitcast.1, bf16[1024,768]{1,0:T(8,128)(2,1)} %c_hbm.1), custom_call_target="tpu_custom_call" | custom-call | tf_op jit(solution)/shard_map/pallas_call | solution.py:406
  200.4 7.9 %copy.4 = f32[1024,2048]{1,0:T(8,128)} copy(f32[1024,2048]{1,0:T(8,128)} %shard_map.28) | data formatting | bytes 16777216

commit v3 on v2

--- a/solution.py
+++ b/solution.py
@@ -11,11 +11,12 @@
 CHUNK = 128
 TILE = 256
 PARTS = 4
-
-
-def kernel(aux, rows_axis, b_hbm, c_hbm, out_hbm, b, c, h, k_acc, h_acc, *sems):
+TRANSIT = 6
+
+
+def kernel(aux, rows_axis, b_hbm, c_hbm, k_acc, b, c, h, t, h_acc, *sems):
     (local_b, local_c, cz_s, cz_r, cy_s, cy_r, cx_s, cx_r,
-     hx_s, hx_r, hz_s, hz_r, hy_s, hy_r, out_sem) = sems
+     hx_s, hx_r, hz_s, hz_r, hy_s, hy_r, ty_s, tz_s, tx_s, t_r) = sems
     span = rows_axis // aux
     chunks, _, n_rows, width = c.shape
     share = n_rows // aux
@@ -37,6 +38,25 @@
     owner = layer == p
     own_slot = jnp.where(owner, 0, 1 + member)
 
+    half = aux // 2
+    partner = jnp.bitwise_xor(p, half)
+    first_transit, first_own = half * PARTS, (half + 1) * PARTS
+    last_transit = first_transit + TRANSIT
+
+    def ahead(index):
+        return jnp.where(index < half, layer - index, index - layer)
+
+    main_far, transit_far = ahead(p), ahead(partner)
+    main_up, transit_way = p < half, jnp.where(partner < half, 1, 0)
+    transit_row = row_of(layer + 2 * transit_way - 1, member)
+    transit_on = jnp.logical_and(transit_far >= 0, jnp.where(partner < half, layer + 1 < aux, layer > 0))
+
+    def own_by_transit(i):
+        return jnp.logical_and(i >= first_own, i < last_transit)
+
+    def other_by_transit(i):
+        return jnp.logical_and(main_far >= 0, jnp.logical_and(i >= first_transit, i < first_own))
+
     def to_row(row):
         return {"device_id": {"row": row}, "device_id_type": MESH}
 
@@ -77,6 +97,8 @@
             **to_aux(jnp.bitwise_xor(p, bit)))
 
     part = n_rows // PARTS
+    slots = aux * PARTS
+    pieces = slots // 2
 
     def message(slot, j, i):
         rows = pl.ds(pl.multiple_of(lax.rem(i, PARTS) * part, part), part)
@@ -87,9 +109,12 @@
             message(own_slot, j, i), message(1 + member, j, i), hz_s.at[way, j], hz_r.at[j, i],
             **to_row(row_of(layer + 2 * way - 1, member)))
 
-    def h_line_sent(j, way):
-        return pltpu.make_async_remote_copy(
-            h.at[0, j], h.at[0, j], hz_s.at[way, j], hz_r.at[j, 0], **to_row(row_of(layer + 2 * way - 1, member)))
+    def messages(j, count):
+        return h.at[0, j, pl.ds(0, n_rows * count // slots)]
+
+    def h_line_sent(j, way, count):
+        return pltpu.make_async_remote_copy(
+            messages(j, count), messages(j, count), hz_s.at[way, j], hz_r.at[j, 0], **to_row(row_of(layer + 2 * way - 1, member)))
 
     def h_member(j, i, step):
         line = lax.rem(member + span - step, span)
@@ -98,9 +123,31 @@
             message(slot, j, i), message(1 + line, j, i), hy_s.at[j, step], hy_r.at[j, step, i],
             **to_row(next_member))
 
-    def h_member_sent(j, step):
-        return pltpu.make_async_remote_copy(
-            h.at[0, j], h.at[0, j], hy_s.at[j, step], hy_r.at[j, step, 0], **to_row(next_member))
+    def h_member_sent(j, step, count):
+        return pltpu.make_async_remote_copy(
+            messages(j, count), messages(j, count), hy_s.at[j, step], hy_r.at[j, step, 0], **to_row(next_member))
+
+    def t_member(j, i):
+        return pltpu.make_async_remote_copy(
+            message(0, j, i), t.at[j, i], ty_s.at[j], t_r.at[j, i], **to_row(next_member))
+
+    def t_line(source, j, i):
+        return pltpu.make_async_remote_copy(source, t.at[j, i], tz_s.at[j], t_r.at[j, i], **to_row(transit_row))
+
+    def t_other(j, i):
+        at = first_transit + i
+        return pltpu.make_async_remote_copy(
+            t.at[j, i], message(1 + lax.rem(member + span - 1, span), j, at), tx_s.at[j], hy_r.at[j, 0, at],
+            **to_aux(partner))
+
+    def t_own(j, i):
+        at = first_transit + i
+        return pltpu.make_async_remote_copy(
+            t.at[j, i], message(1 + member, j, at), tx_s.at[j], hz_r.at[j, at], **to_aux(partner))
+
+    def t_sent(j, count, sem, where):
+        some = t.at[j, pl.ds(0, count)]
+        return pltpu.make_async_remote_copy(some, some, sem.at[j], t_r.at[j, 0], **where)
 
     up, down = layer + 1 < aux, layer > 0
 
@@ -191,9 +238,6 @@
             for bit in lower(k):
                 c_aux(j, k, bit).start()
 
-    slots = aux * PARTS
-    pieces = slots // 2
-
     def transform(j, piece):
         @pl.when(piece == 0)
         def _():
@@ -212,6 +256,10 @@
             for bit in bits:
                 h_aux(j, 0, bit).start()
 
+            @pl.when(transit_far == 0)
+            def _():
+                loop(PARTS, lambda i: t_member(j, i).start())
+
             @pl.when(j > 0)
             def _():
                 send_rest(j - 1)
@@ -221,20 +269,26 @@
             @pl.when(j + 2 < chunks)
             def _():
                 spread_c(j + 2)
+
+    def pass_member(j, i):
+        @pl.when(jnp.logical_not(other_by_transit(i)))
+        def _():
+            h_member(j, i, 0).start()
+
+    def pass_line(j, i, way):
+        is_far = main_up if way else jnp.logical_not(main_up)
+
+        @pl.when(jnp.logical_and(up if way else down, jnp.logical_not(jnp.logical_and(is_far, own_by_transit(i)))))
+        def _():
+            h_line(j, i, way).start()
 
     def send_h(j, k):
         @pl.when(owner)
         def _():
             def send(i):
-                @pl.when(up)
-                def _():
-                    h_line(j, i, 1).start()
-
-                @pl.when(down)
-                def _():
-                    h_line(j, i, 0).start()
-
-                h_member(j, i, 0).start()
+                pass_line(j, i, 1)
+                pass_line(j, i, 0)
+                pass_member(j, i)
 
             loop_from(k * PARTS, (k + 1) * PARTS, send)
 
@@ -257,30 +311,42 @@
         @pl.when(layer > p)
         def _():
             h_line(j, i, 1).wait_recv()
-
-            @pl.when(up)
-            def _():
-                h_line(j, i, 1).start()
-
-            h_member(j, i, 0).start()
+            pass_line(j, i, 1)
+            pass_member(j, i)
 
         @pl.when(layer < p)
         def _():
             h_line(j, i, 0).wait_recv()
-
-            @pl.when(down)
-            def _():
-                h_line(j, i, 0).start()
-
-            h_member(j, i, 0).start()
+            pass_line(j, i, 0)
+            pass_member(j, i)
+
+    def relay_t(j, i):
+        is_first = transit_far == 0
+        is_other = i < PARTS
+
+        @pl.when(jnp.logical_or(transit_far > 0, jnp.logical_and(is_first, is_other)))
+        def _():
+            t_line(t.at[j, i], j, i).wait_recv()
+
+            @pl.when(transit_on)
+            def _():
+                t_line(t.at[j, i], j, i).start()
+
+            @pl.when(is_other)
+            def _():
+                t_other(j, i).start()
+
+            @pl.when(jnp.logical_not(is_other))
+            def _():
+                t_own(j, i).start()
+
+        @pl.when(jnp.logical_and(jnp.logical_and(is_first, transit_on), jnp.logical_not(is_other)))
+        def _():
+            t_line(message(0, j, i), j, i).start()
 
     tile = min(TILE, n_rows)
     tiles = n_rows // tile
     all_tiles = span * tiles
-
-    def out_copy(n):
-        columns = pl.ds(pl.multiple_of(n * tile, tile), tile)
-        return pltpu.make_async_copy(k_acc.at[:, columns], out_hbm.at[:, columns], out_sem.at[n])
 
     def take_members(j, first, last):
         for step in range(span - 1):
@@ -313,7 +379,6 @@
 
         def finish(n):
             add_tile(j, n, aux - 1, aux)
-            out_copy(n).start()
 
         loop(all_tiles, finish)
 
@@ -334,11 +399,29 @@
     load_b.wait()
     loop(pieces, lambda piece: transform(0, piece))
 
+    @pl.when(transit_far == 0)
+    def _():
+        loop(TRANSIT, lambda i: relay_t(0, i))
+
     quarter = slots // 4
 
     def main(j):
         def slot(i):
             relay_h(j, i)
+
+            turn = j * slots + i + slots - pieces - TRANSIT * transit_far
+            opening = i - jnp.minimum(TRANSIT * (transit_far - 1), slots - TRANSIT)
+            is_opening = jnp.logical_and(
+                jnp.logical_and(j == 0, transit_far > 0), jnp.logical_and(opening >= 0, opening < TRANSIT))
+            t_chunk = jnp.where(is_opening, 0, lax.div(jnp.maximum(turn, 0), slots))
+            t_message = jnp.where(is_opening, opening, lax.rem(jnp.maximum(turn, 0), slots))
+            t_now = jnp.logical_or(is_opening, jnp.logical_and(
+                jnp.logical_and(turn >= slots, t_chunk < chunks), t_message < TRANSIT))
+
+            @pl.when(jnp.logical_and(t_now, transit_far >= 0))
+            def _():
+                relay_t(t_chunk, t_message)
+
             early = jnp.logical_and(j == 1, i < quarter)
             chunk = jnp.where(j == 0, jnp.where(i < pieces, 1, 2), jnp.where(early, 2, j + 2))
             piece = jnp.where(
@@ -379,19 +462,43 @@
             c_aux(j, k ^ low, low).wait_send()
             h_aux(j, k ^ low, low).wait_send()
 
-        @pl.when(jnp.logical_and(up, layer >= p))
-        def _():
-            h_line_sent(j, 1).wait_send()
-
-        @pl.when(jnp.logical_and(down, layer <= p))
-        def _():
-            h_line_sent(j, 0).wait_send()
-
-        for step in range(span - 1):
-            h_member_sent(j, step).wait_send()
+        own_kept = slots - (last_transit - first_own)
+        for way, has_next, sends in ((1, up, layer >= p), (0, down, layer <= p)):
+            is_far = main_up if way else jnp.logical_not(main_up)
+
+            @pl.when(jnp.logical_and(jnp.logical_and(has_next, sends), is_far))
+            def _():
+                h_line_sent(j, way, own_kept).wait_send()
+
+            @pl.when(jnp.logical_and(jnp.logical_and(has_next, sends), jnp.logical_not(is_far)))
+            def _():
+                h_line_sent(j, way, slots).wait_send()
+
+        @pl.when(main_far >= 0)
+        def _():
+            h_member_sent(j, 0, slots - PARTS).wait_send()
+
+        @pl.when(main_far < 0)
+        def _():
+            h_member_sent(j, 0, slots).wait_send()
+
+        for step in range(1, span - 1):
+            h_member_sent(j, step, slots).wait_send()
+
+        @pl.when(transit_far == 0)
+        def _():
+            t_sent(j, PARTS, ty_s, to_row(next_member)).wait_send()
+            t_sent(j, PARTS, tx_s, to_aux(partner)).wait_send()
+
+        @pl.when(transit_far > 0)
+        def _():
+            t_sent(j, TRANSIT, tx_s, to_aux(partner)).wait_send()
+
+        @pl.when(transit_on)
+        def _():
+            t_sent(j, TRANSIT, tz_s, to_row(transit_row)).wait_send()
 
     loop(chunks, drain)
-    loop(all_tiles, lambda n: out_copy(n).wait())
 
 
 def body(aux, rows_axis, integrals, orbitals):
@@ -405,14 +512,14 @@
     steps = max(span - 1, 1)
     return pl.pallas_call(
         functools.partial(kernel, aux, rows_axis),
-        out_shape=jax.ShapeDtypeStruct((n_rows, span * n_rows), jnp.float32),
+        out_shape=pltpu.VMEM((n_rows, span * n_rows), jnp.float32),
         in_specs=[pl.BlockSpec(memory_space=pl.ANY)] * 2,
-        out_specs=pl.BlockSpec(memory_space=pl.ANY),
+        out_specs=pl.BlockSpec(memory_space=pltpu.VMEM),
         scratch_shapes=[
             pltpu.VMEM((n_rows, n), integrals.dtype),
             pltpu.VMEM((chunks, rows_axis, n_rows, width), orbitals.dtype),
             pltpu.VMEM((1 + span, chunks, n_rows, aux * width), jnp.bfloat16),
-            pltpu.VMEM((n_rows, span * n_rows), jnp.float32),
+            pltpu.VMEM((chunks, TRANSIT, n_rows // PARTS, width), jnp.bfloat16),
             pltpu.VMEM((n_rows, width), jnp.float32),
             dma, dma((chunks,)),
             dma((2, chunks, aux)), dma((chunks, aux)),
@@ -421,10 +528,10 @@
             dma((chunks, aux)), dma((chunks, aux)),
             dma((2, chunks)), dma((chunks, aux * PARTS)),
             dma((chunks, steps)), dma((chunks, steps, aux * PARTS)),
-            dma((tiles,)),
+            dma((chunks,)), dma((chunks,)), dma((chunks,)), dma((chunks, TRANSIT)),
         ],
         compiler_params=pltpu.CompilerParams(
-            collective_id=0, has_side_effects=True, vmem_limit_bytes=67_043_328),
+            collective_id=0, has_side_effects=True, vmem_limit_bytes=54 * 2**20),
     )(integrals.reshape(n_rows, n), orbitals)
 
 

time: 208 us -> 223 us (1.072); the launches traced: 208 us -> 221 us
  Pallas kernels: 200 us -> 217 us
  local copies, waits for them, and re-layouts: 7.89 us -> 3.4 us
    pallas_call x1, Pallas kernels: 200 us -> 217 us  [body(): pl.pallas_call(functools.partial(kernel, aux, rows_axis), out_shape=pltpu...]
    unnamed x1, local copies, waits for them, and re-layouts: 7.89 us -> 3.4 us
where the time goes in v3:
time: 223 us; the launch traced here: 221 us
  Pallas kernels  217 us (97%)
  local copies, waits for them, and re-layouts  3.4 us (2%)
    pallas_call x1, Pallas kernels, body(): pl.pallas_call(functools.partial(kernel, aux, rows_axis), out_shape=pltpu...  217 us

profile of v3, /device:TPU:2, one launch (start us, length us, event | category | flops | bytes accessed | tf_op | source)
XLA Modules:
  0.0 220.8 jit_solution(10154669849606922559)
XLA Ops:
  0.0 217.4 %shard_map.28 = f32[1024,2048]{1,0:T(8,128)S(1)} custom-call(bf16[1024,8192]{1,0:T(8,128)(2,1)} %bitcast.1, bf16[1024,768]{1,0:T(8,128)(2,1)} %c_hbm.1), custom_call_target="tpu_custom_call" | custom-call | tf_op jit(solution)/shard_map/pallas_call | solution.py:513
  217.4 3.4 %copy.4 = f32[1024,2048]{1,0:T(8,128)} copy(f32[1024,2048]{1,0:T(8,128)S(1)} %shard_map.28) | data formatting | bytes 16777216

commit v4 on v2

v4 whole, which is shorter than its diff:
```python
import functools

import jax
import jax.numpy as jnp
from jax import lax
from jax.experimental import pallas as pl
from jax.experimental.pallas import tpu as pltpu
from jax.sharding import PartitionSpec as P

MESH = pl.DeviceIdType.MESH
CHUNK = 128
TILE = 256
PARTS = 4


def kernel(aux, rows_axis, b_hbm, c_hbm, k_acc, b, c, h, h_acc, *sems):
    (local_b, local_c, cz_s, cz_r, cy_s, cy_r, cx_s, cx_r,
     hx_s, hx_r, hz_s, hz_r, hy_s, hy_r) = sems
    span = rows_axis // aux
    chunks, _, _, n_rows, width = c.shape
    share = n_rows // aux
    p = lax.axis_index("aux")
    r = lax.axis_index("row")
    layer = lax.div(r, span)
    member = lax.rem(r, span)
    bits = []
    bit = aux // 2
    while bit:
        bits.append(bit)
        bit //= 2

    def row_of(at_layer, at_member):
        return at_layer * span + at_member

    next_member = row_of(layer, lax.rem(member + 1, span))
    last_member = row_of(layer, lax.rem(member + span - 1, span))
    owner = layer == p
    own_slot = jnp.where(owner, 0, 1 + member)

    def to_row(row):
        return {"device_id": {"row": row}, "device_id_type": MESH}

    def to_aux(index):
        return {"device_id": {"aux": index}, "device_id_type": MESH}

    def lower(k):
        low = k & -k if k else aux
        return [bit for bit in bits if bit < low]

    def quarter_of(index):
        return pl.ds(pl.multiple_of(index * share, share), share)

    def c_piece(j, at_layer, at_member):
        return c.at[j, at_layer, at_member, quarter_of(p)]

    def c_line(j, at_layer, way):
        piece = c_piece(j, at_layer, member)
        return pltpu.make_async_remote_copy(
            piece, piece, cz_s.at[way], cz_r.at[j, at_layer], **to_row(row_of(layer + 2 * way - 1, member)))

    def c_line_sent(way, count):
        some = c.at[:, 0, 0, pl.ds(0, count * share)]
        return pltpu.make_async_remote_copy(
            some, some, cz_s.at[way], cz_r.at[0, 0], **to_row(row_of(layer + 2 * way - 1, member)))

    def c_member(j, at_layer, step):
        piece = c_piece(j, at_layer, lax.rem(member + span - step, span))
        return pltpu.make_async_remote_copy(
            piece, piece, cy_s.at[step], cy_r.at[j, step], **to_row(next_member))

    def c_members(j, step):
        pieces = c.at[j, :, 0, quarter_of(p)]
        return pltpu.make_async_remote_copy(
            pieces, pieces, cy_s.at[step], cy_r.at[j, step], **to_row(next_member))

    def c_members_sent(step):
        some = c.at[:, 0, 0]
        return pltpu.make_async_remote_copy(some, some, cy_s.at[step], cy_r.at[0, step], **to_row(next_member))

    def c_aux_copy(piece, j, k, bit):
        return pltpu.make_async_remote_copy(
            piece, piece, cx_s, cx_r.at[j, k ^ bit], **to_aux(jnp.bitwise_xor(p, bit)))

    def c_aux_piece(j, at_layer, bit):
        return c_aux_copy(c_piece(j, at_layer, member), j, 0, bit)

    def c_aux_members(j, at_member, bit):
        return c_aux_copy(c.at[j, :, at_member, quarter_of(p)], j, 0, bit)

    def c_aux(j, k, bit):
        return c_aux_copy(c.at[j, :, :, quarter_of(jnp.bitwise_xor(p, k))], j, k, bit)

    def c_aux_sent():
        some = c.at[:, :, :, pl.ds(0, (aux - 1) * share)]
        return pltpu.make_async_remote_copy(some, some, cx_s, cx_r.at[0, 0], **to_aux(jnp.bitwise_xor(p, 1)))

    def lanes(k):
        return pl.ds(k * width, width)

    def h_aux(j, k, bit):
        return pltpu.make_async_remote_copy(
            h.at[0, j, :, lanes(k)], h.at[0, j, :, lanes(k ^ bit)], hx_s, hx_r.at[j, k ^ bit],
            **to_aux(jnp.bitwise_xor(p, bit)))

    def h_aux_sent():
        some = h.at[0, :, :, pl.ds(0, (aux - 1) * width)]
        return pltpu.make_async_remote_copy(some, some, hx_s, hx_r.at[0, 0], **to_aux(jnp.bitwise_xor(p, 1)))

    part = n_rows // PARTS
    slots = aux * PARTS
    pieces = slots // 2

    def message(slot, j, i):
        rows = pl.ds(pl.multiple_of(lax.rem(i, PARTS) * part, part), part)
        return h.at[slot, j, rows, pl.ds(pl.multiple_of(lax.div(i, PARTS) * width, width), width)]

    def h_line(j, i, way):
        return pltpu.make_async_remote_copy(
            message(own_slot, j, i), message(1 + member, j, i), hz_s.at[way], hz_r.at[j, i],
            **to_row(row_of(layer + 2 * way - 1, member)))

    def h_line_sent(way):
        return pltpu.make_async_remote_copy(
            h.at[0], h.at[0], hz_s.at[way], hz_r.at[0, 0], **to_row(row_of(layer + 2 * way - 1, member)))

    def h_member(j, i, step):
        line = lax.rem(member + span - step, span)
        slot = own_slot if step == 0 else 1 + line
        return pltpu.make_async_remote_copy(
            message(slot, j, i), message(1 + line, j, i), hy_s.at[step], hy_r.at[j, step, lax.div(i, pieces)],
            **to_row(next_member))

    def h_members(j, half, step):
        some = h.at[0, j, :, pl.ds(0, aux // 2 * width)]
        return pltpu.make_async_remote_copy(some, some, hy_s.at[step], hy_r.at[j, step, half], **to_row(next_member))

    def h_member_sent(step):
        return pltpu.make_async_remote_copy(
            h.at[0], h.at[0], hy_s.at[step], hy_r.at[0, step, 0], **to_row(next_member))

    up, down = layer + 1 < aux, layer > 0

    barrier = pltpu.get_barrier_semaphore()
    for bit in bits:
        pl.semaphore_signal(barrier, 1, **to_aux(jnp.bitwise_xor(p, bit)))
    pl.semaphore_signal(barrier, 1, **to_row(next_member))
    pl.semaphore_signal(barrier, 1, **to_row(last_member))

    @pl.when(up)
    def _():
        pl.semaphore_signal(barrier, 1, **to_row(row_of(layer + 1, member)))

    @pl.when(down)
    def _():
        pl.semaphore_signal(barrier, 1, **to_row(row_of(layer - 1, member)))

    def own_c(j):
        return pltpu.make_async_copy(
            c_hbm.at[pl.ds(pl.multiple_of(p * share, share), share), pl.ds(pl.multiple_of(j * width, width), width)],
            c_piece(j, layer, member), local_c.at[j])

    for j in range(chunks):
        own_c(j).start()
    load_b = pltpu.make_async_copy(b_hbm, b, local_b)
    load_b.start()
    pl.semaphore_wait(barrier, len(bits) + 2 + up.astype(jnp.int32) + down.astype(jnp.int32))

    def loop_from(first, last, body):
        def step(i, carry):
            body(i)
            return carry
        lax.fori_loop(first, last, step, 0)

    def loop(count, body):
        loop_from(0, count, body)

    def pass_c(j, at_layer, spread):
        c_member(j, at_layer, 0).start()
        if spread:
            for bit in bits:
                c_aux_piece(j, at_layer, bit).start()

    def start_c(j, spread=False):
        own_c(j).wait()

        @pl.when(up)
        def _():
            c_line(j, layer, 1).start()

        @pl.when(down)
        def _():
            c_line(j, layer, 0).start()

        pass_c(j, layer, spread)

    def relay_c(j, spread=False):
        for step in range(1, aux):
            @pl.when(layer - step >= 0)
            def _():
                c_line(j, layer - step, 1).wait_recv()

                @pl.when(up)
                def _():
                    c_line(j, layer - step, 1).start()

                pass_c(j, layer - step, spread)

            @pl.when(layer + step < aux)
            def _():
                c_line(j, layer + step, 0).wait_recv()

                @pl.when(down)
                def _():
                    c_line(j, layer + step, 0).start()

                pass_c(j, layer + step, spread)

    def spread_c(j, spread=False):
        if not spread:
            for bit in bits:
                c_aux_members(j, member, bit).start()
        for step in range(span - 1):
            c_members(j, step).wait_recv()
            if step + 1 < span - 1:
                for at_layer in range(aux):
                    c_member(j, at_layer, step + 1).start()
            for bit in bits:
                c_aux_members(j, lax.rem(member + span - 1 - step, span), bit).start()

    def finish_c(j):
        for k in sorted(range(1, aux), key=lambda k: -(k & -k)):
            c_aux(j, k ^ (k & -k), k & -k).wait_recv()
            for bit in lower(k):
                c_aux(j, k, bit).start()

    slots = aux * PARTS
    pieces = slots // 2

    def transform(j, piece):
        @pl.when(piece == 0)
        def _():
            finish_c(j)
            h_acc[...] = jnp.zeros_like(h_acc)

        def block(i):
            h_acc[...] += jnp.dot(
                b[:, pl.ds(pl.multiple_of(i * n_rows, n_rows), n_rows)], c[j, lax.div(i, span), lax.rem(i, span)],
                preferred_element_type=jnp.float32)

        loop_from(lax.div(piece * rows_axis, pieces), lax.div((piece + 1) * rows_axis, pieces), block)

        @pl.when(piece == pieces - 1)
        def _():
            h[0, j, :, lanes(0)] = h_acc[...].astype(h.dtype)
            for bit in bits:
                h_aux(j, 0, bit).start()

            @pl.when(j > 0)
            def _():
                send_rest(j - 1)

            send_first(j)

            @pl.when(j + 2 < chunks)
            def _():
                spread_c(j + 2)

    def send_h(j, k):
        @pl.when(owner)
        def _():
            def send(i):
                @pl.when(up)
                def _():
                    h_line(j, i, 1).start()

                @pl.when(down)
                def _():
                    h_line(j, i, 0).start()

                h_member(j, i, 0).start()

            loop_from(k * PARTS, (k + 1) * PARTS, send)

    def take_h(j, k):
        h_aux(j, k ^ (k & -k), k & -k).wait_recv()
        for bit in lower(k):
            h_aux(j, k, bit).start()
        send_h(j, k)

    def send_first(j):
        send_h(j, 0)
        for k in range(1, aux // 2):
            take_h(j, k)

    def send_rest(j):
        for k in range(aux // 2, aux):
            take_h(j, k)

    def relay_h(j, i):
        @pl.when(layer > p)
        def _():
            h_line(j, i, 1).wait_recv()

            @pl.when(up)
            def _():
                h_line(j, i, 1).start()

            h_member(j, i, 0).start()

        @pl.when(layer < p)
        def _():
            h_line(j, i, 0).wait_recv()

            @pl.when(down)
            def _():
                h_line(j, i, 0).start()

            h_member(j, i, 0).start()

    tile = min(TILE, n_rows)
    tiles = n_rows // tile
    all_tiles = span * tiles

    def take_members(j, half):
        for step in range(span - 1):
            h_members(j, half, step).wait_recv()
            if step + 1 < span - 1:
                loop_from(half * pieces, (half + 1) * pieces, lambda i: h_member(j, i, step + 1).start())

    def add_tile(j, n, first, last):
        line = lax.div(n, tiles)
        slot = jnp.where(line == member, own_slot, 1 + line)
        at = pl.ds(pl.multiple_of(lax.rem(n, tiles) * tile, tile), tile)
        some = pl.ds(first * width, (last - first) * width)
        k_acc[:, pl.ds(pl.multiple_of(n * tile, tile), tile)] += lax.dot_general(
            h[0, j, :, some], h[slot, j, at, some], (((1,), (1,)), ((), ())), preferred_element_type=jnp.float32)

    def update(j, piece, count, halves):
        @pl.when(piece == 0)
        def _():
            for half in halves:
                take_members(j, half)

        loop_from(lax.div(piece * all_tiles, count), lax.div((piece + 1) * all_tiles, count),
                  lambda n: add_tile(j, n, halves[0] * (aux // 2), (halves[-1] + 1) * (aux // 2)))

    def last_update(j):
        def own(n):
            add_tile(j, member * tiles + n, aux // 2, aux)

        def other(n):
            add_tile(j, lax.rem(member * tiles + n, all_tiles), aux // 2, aux)

        loop(tiles, own)
        take_members(j, 1)
        loop_from(tiles, all_tiles, other)

    start_c(0, True)
    start_c(1, True)

    def clear(n):
        columns = pl.ds(pl.multiple_of(n * tile, tile), tile)
        k_acc[:, columns] = jnp.zeros((n_rows, tile), jnp.float32)

    loop(span * tiles, clear)

    relay_c(0, True)
    start_c(2)
    relay_c(1, True)
    spread_c(0, True)
    start_c(3)
    relay_c(2)
    spread_c(1, True)
    loop_from(4, chunks, start_c)
    relay_c(3)
    load_b.wait()
    loop(pieces // 2, lambda piece: transform(0, piece))
    loop_from(4, chunks - 1, relay_c)
    loop_from(pieces // 2, pieces, lambda piece: transform(0, piece))
    loop_from(max(4, chunks - 1), chunks, relay_c)

    quarter = slots // 4

    def main(j):
        def slot(i):
            relay_h(j, i)
            early = jnp.logical_and(j == 1, i < quarter)
            chunk = jnp.where(j == 0, jnp.where(i < pieces, 1, 2), jnp.where(early, 2, j + 2))
            piece = jnp.where(
                j == 0, jnp.where(i < pieces, i, i - 3 * quarter), jnp.where(early, i + quarter, i - quarter))
            now = jnp.logical_and(jnp.logical_and(piece >= 0, piece < pieces), chunk < chunks)

            @pl.when(now)
            def _():
                transform(chunk, piece)

            @pl.when(jnp.logical_and(jnp.logical_and(j > 0, j < chunks - 2), i >= 3 * quarter))
            def _():
                update(j - 1, i - 3 * quarter, quarter, (0, 1))

            @pl.when(jnp.logical_and(j >= chunks - 2, jnp.logical_and(i >= quarter, i < 3 * quarter)))
            def _():
                update(j - 1, i - quarter, pieces, (0, 1))

            @pl.when(jnp.logical_and(j == chunks - 1, i >= 3 * quarter))
            def _():
                update(j, i - 3 * quarter, quarter, (0,))

        loop(slots, slot)

        @pl.when(j == max(chunks - 2, 0))
        def _():
            send_rest(chunks - 1)

    loop(chunks, main)
    last_update(chunks - 1)

    for at in range(aux):
        @pl.when(layer == at)
        def _():
            if at + 1 < aux:
                c_line_sent(1, at + 1).wait_send()
            if at > 0:
                c_line_sent(0, aux - at).wait_send()
    c_aux_sent().wait_send()
    h_aux_sent().wait_send()
    for step in range(span - 1):
        c_members_sent(step).wait_send()
        h_member_sent(step).wait_send()

    @pl.when(jnp.logical_and(up, layer >= p))
    def _():
        h_line_sent(1).wait_send()

    @pl.when(jnp.logical_and(down, layer <= p))
    def _():
        h_line_sent(0).wait_send()


def body(aux, rows_axis, integrals, orbitals):
    _, n_rows, n = integrals.shape
    occ = orbitals.shape[1]
    span = rows_axis // aux
    width = CHUNK
    chunks = occ // width
    dma = pltpu.SemaphoreType.DMA
    tiles = span * (n_rows // min(TILE, n_rows))
    steps = max(span - 1, 1)
    return pl.pallas_call(
        functools.partial(kernel, aux, rows_axis),
        out_shape=pltpu.VMEM((n_rows, span * n_rows), jnp.float32),
        in_specs=[pl.BlockSpec(memory_space=pl.ANY)] * 2,
        out_specs=pl.BlockSpec(memory_space=pltpu.VMEM),
        scratch_shapes=[
            pltpu.VMEM((n_rows, n), integrals.dtype),
            pltpu.VMEM((chunks, aux, span, n_rows, width), orbitals.dtype),
            pltpu.VMEM((1 + span, chunks, n_rows, aux * width), jnp.bfloat16),
            pltpu.VMEM((n_rows, width), jnp.float32),
            dma, dma((chunks,)),
            dma((2,)), dma((chunks, aux)),
            dma((steps,)), dma((chunks, steps)),
            dma, dma((chunks, aux)),
            dma, dma((chunks, aux)),
            dma((2,)), dma((chunks, aux * PARTS)),
            dma((steps,)), dma((chunks, steps, 2)),
        ],
        compiler_params=pltpu.CompilerParams(
            collective_id=0, has_side_effects=True, vmem_limit_bytes=54 * 2**20),
    )(integrals.reshape(n_rows, n), orbitals)


def solution(mesh):
    aux, rows_axis = mesh.shape["aux"], mesh.shape["row"]
    return jax.shard_map(
        functools.partial(body, aux, rows_axis), mesh=mesh,
        in_specs=(P("aux", "row", None), P("row", None)), out_specs=P("row", "aux"), check_vma=False)
```

time: 208 us -> 199 us (0.957)
  local copies, waits for them, and re-layouts: 7.89 us -> 3.4 us
  Pallas kernels: 200 us -> 196 us
    unnamed x1, local copies, waits for them, and re-layouts: 7.89 us -> 3.4 us
    pallas_call x1, Pallas kernels: 200 us -> 196 us  [body(): pl.pallas_call(functools.partial(kernel, aux, rows_axis), out_shape=pltpu...]
where the time goes in v4:
time: 199 us
  Pallas kernels  196 us (98%)
  local copies, waits for them, and re-layouts  3.4 us (2%)
    pallas_call x1, Pallas kernels, body(): pl.pallas_call(functools.partial(kernel, aux, rows_axis), out_shape=pltpu...  196 us

profile of v4, /device:TPU:2, one launch (start us, length us, event | category | flops | bytes accessed | tf_op | source)
XLA Modules:
  0.0 199.3 jit_solution(5899779700643302446)
XLA Ops:
  0.0 195.9 %shard_map.28 = f32[1024,2048]{1,0:T(8,128)S(1)} custom-call(bf16[1024,8192]{1,0:T(8,128)(2,1)} %bitcast.1, bf16[1024,768]{1,0:T(8,128)(2,1)} %c_hbm.1), custom_call_target="tpu_custom_call" | custom-call | tf_op jit(solution)/shard_map/pallas_call | solution.py:449
  195.9 3.4 %copy.4 = f32[1024,2048]{1,0:T(8,128)} copy(f32[1024,2048]{1,0:T(8,128)S(1)} %shard_map.28) | data formatting | bytes 16777216

commit v5 on v4

--- a/solution.py
+++ b/solution.py
@@ -11,11 +11,13 @@
 CHUNK = 128
 TILE = 256
 PARTS = 4
-
-
-def kernel(aux, rows_axis, b_hbm, c_hbm, k_acc, b, c, h, h_acc, *sems):
+REST = 5
+TRANSIT_FROM = 3
+
+
+def kernel(aux, rows_axis, b_hbm, c_hbm, k_acc, b, c, h, t, h_acc, *sems):
     (local_b, local_c, cz_s, cz_r, cy_s, cy_r, cx_s, cx_r,
-     hx_s, hx_r, hz_s, hz_r, hy_s, hy_r) = sems
+     hx_s, hx_r, hz_s, hz_r, hy_s, hy_r, td_s, ty_s, t_r) = sems
     span = rows_axis // aux
     chunks, _, _, n_rows, width = c.shape
     share = n_rows // aux
@@ -37,6 +39,19 @@
     owner = layer == p
     own_slot = jnp.where(owner, 0, 1 + member)
 
+    half = aux // 2
+    partner = jnp.bitwise_xor(p, half)
+    t_from = TRANSIT_FROM
+
+    def ahead(index):
+        return jnp.where(index < half, layer - index, index - layer)
+
+    main_far, transit_far = ahead(p), ahead(partner)
+    main_up = p < half
+
+    def is_far_way(way):
+        return main_up if way else jnp.logical_not(main_up)
+
     def to_row(row):
         return {"device_id": {"row": row}, "device_id_type": MESH}
 
@@ -58,8 +73,17 @@
         return pltpu.make_async_remote_copy(
             piece, piece, cz_s.at[way], cz_r.at[j, at_layer], **to_row(row_of(layer + 2 * way - 1, member)))
 
+    def c_direct(at_layer):
+        piece = c_piece(0, layer, member)
+        return pltpu.make_async_remote_copy(
+            piece, piece, cz_s.at[2], cz_r.at[0, layer], **to_row(row_of(at_layer, member)))
+
+    def c_direct_sent():
+        some = c.at[0, 0, 0, pl.ds(0, (aux - 1) * share)]
+        return pltpu.make_async_remote_copy(some, some, cz_s.at[2], cz_r.at[0, 0], **to_row(next_member))
+
     def c_line_sent(way, count):
-        some = c.at[:, 0, 0, pl.ds(0, count * share)]
+        some = c.at[pl.ds(1, chunks - 1), 0, 0, pl.ds(0, count * share)]
         return pltpu.make_async_remote_copy(
             some, some, cz_s.at[way], cz_r.at[0, 0], **to_row(row_of(layer + 2 * way - 1, member)))
 
@@ -77,22 +101,24 @@
         some = c.at[:, 0, 0]
         return pltpu.make_async_remote_copy(some, some, cy_s.at[step], cy_r.at[0, step], **to_row(next_member))
 
-    def c_aux_copy(piece, j, k, bit):
-        return pltpu.make_async_remote_copy(
-            piece, piece, cx_s, cx_r.at[j, k ^ bit], **to_aux(jnp.bitwise_xor(p, bit)))
+    def c_aux_copy(piece, j, others, k, bit):
+        return pltpu.make_async_remote_copy(
+            piece, piece, cx_s, cx_r.at[j, others, k ^ bit], **to_aux(jnp.bitwise_xor(p, bit)))
 
     def c_aux_piece(j, at_layer, bit):
-        return c_aux_copy(c_piece(j, at_layer, member), j, 0, bit)
-
-    def c_aux_members(j, at_member, bit):
-        return c_aux_copy(c.at[j, :, at_member, quarter_of(p)], j, 0, bit)
-
-    def c_aux(j, k, bit):
-        return c_aux_copy(c.at[j, :, :, quarter_of(jnp.bitwise_xor(p, k))], j, k, bit)
+        return c_aux_copy(c_piece(j, at_layer, member), j, 0, 0, bit)
+
+    def c_aux_members(j, step, k, bit):
+        at_member = lax.rem(member + span - step, span)
+        return c_aux_copy(c.at[j, :, at_member, quarter_of(jnp.bitwise_xor(p, k))], j, int(step > 0), k, bit)
+
+    def c_aux_all(j, others, k, bit):
+        some = c.at[j, :, pl.ds(0, span - 1 if others else 1), quarter_of(p)]
+        return c_aux_copy(some, j, others, k, bit)
 
     def c_aux_sent():
         some = c.at[:, :, :, pl.ds(0, (aux - 1) * share)]
-        return pltpu.make_async_remote_copy(some, some, cx_s, cx_r.at[0, 0], **to_aux(jnp.bitwise_xor(p, 1)))
+        return pltpu.make_async_remote_copy(some, some, cx_s, cx_r.at[0, 0, 0], **to_aux(jnp.bitwise_xor(p, 1)))
 
     def lanes(k):
         return pl.ds(k * width, width)
@@ -114,45 +140,88 @@
         rows = pl.ds(pl.multiple_of(lax.rem(i, PARTS) * part, part), part)
         return h.at[slot, j, rows, pl.ds(pl.multiple_of(lax.div(i, PARTS) * width, width), width)]
 
+    def late(j):
+        return int(j >= t_from) if isinstance(j, int) else (j >= t_from).astype(jnp.int32)
+
+    def by_transit(j, i):
+        return jnp.logical_and(j >= t_from, jnp.logical_and(i >= half * PARTS, i < (half + 1) * PARTS))
+
     def h_line(j, i, way):
         return pltpu.make_async_remote_copy(
-            message(own_slot, j, i), message(1 + member, j, i), hz_s.at[way], hz_r.at[j, i],
+            message(own_slot, j, i), message(1 + member, j, i), hz_s.at[way, late(j)], hz_r.at[j, i],
             **to_row(row_of(layer + 2 * way - 1, member)))
 
-    def h_line_sent(way):
-        return pltpu.make_async_remote_copy(
-            h.at[0], h.at[0], hz_s.at[way], hz_r.at[0, 0], **to_row(row_of(layer + 2 * way - 1, member)))
+    def h_line_sent(way, is_late, count):
+        some = h.at[0, pl.ds(t_from, chunks - t_from) if is_late else pl.ds(0, t_from), :, pl.ds(0, count * width)]
+        return pltpu.make_async_remote_copy(
+            some, some, hz_s.at[way, is_late], hz_r.at[0, 0], **to_row(row_of(layer + 2 * way - 1, member)))
 
     def h_member(j, i, step):
         line = lax.rem(member + span - step, span)
         slot = own_slot if step == 0 else 1 + line
         return pltpu.make_async_remote_copy(
-            message(slot, j, i), message(1 + line, j, i), hy_s.at[step], hy_r.at[j, step, lax.div(i, pieces)],
+            message(slot, j, i), message(1 + line, j, i), hy_s.at[step, late(j)], hy_r.at[j, step, lax.div(i, pieces)],
             **to_row(next_member))
 
     def h_members(j, half, step):
         some = h.at[0, j, :, pl.ds(0, aux // 2 * width)]
-        return pltpu.make_async_remote_copy(some, some, hy_s.at[step], hy_r.at[j, step, half], **to_row(next_member))
-
-    def h_member_sent(step):
-        return pltpu.make_async_remote_copy(
-            h.at[0], h.at[0], hy_s.at[step], hy_r.at[0, step, 0], **to_row(next_member))
+        return pltpu.make_async_remote_copy(some, some, hy_s.at[step, 0], hy_r.at[j, step, half], **to_row(next_member))
+
+    def h_member_sent(step, is_late, count):
+        some = h.at[0, pl.ds(t_from, chunks - t_from) if is_late else pl.ds(0, t_from), :, pl.ds(0, count * width)]
+        return pltpu.make_async_remote_copy(
+            some, some, hy_s.at[step, is_late], hy_r.at[0, step, 0], **to_row(next_member))
+
+    def t_member(j):
+        return pltpu.make_async_remote_copy(
+            h.at[0, j, :, lanes(0)], t.at[j - t_from], ty_s, t_r.at[j - t_from], **to_row(next_member))
+
+    def t_member_sent():
+        return pltpu.make_async_remote_copy(t, t, ty_s, t_r.at[0], **to_row(next_member))
+
+    def far_layer(distance):
+        return jnp.where(partner < half, partner + distance, partner - distance)
+
+    def to_far(distance):
+        return {"device_id": {"aux": partner, "row": row_of(far_layer(distance), member)}, "device_id_type": MESH}
+
+    def t_own(j, distance):
+        return pltpu.make_async_remote_copy(
+            h.at[0, j, :, lanes(0)], h.at[1 + member, j, :, lanes(half)], td_s.at[j - t_from],
+            hz_r.at[j, half * PARTS], **to_far(distance))
+
+    def t_other(j, distance):
+        return pltpu.make_async_remote_copy(
+            t.at[j - t_from], h.at[1 + lax.rem(member + span - 1, span), j, :, lanes(half)], td_s.at[j - t_from],
+            hy_r.at[j, 0, 1], **to_far(distance))
+
+    def t_sent(j, count):
+        some = h.at[pl.ds(0, 2), 0, :, pl.ds(0, count * width)]
+        return pltpu.make_async_remote_copy(some, some, td_s.at[j - t_from], t_r.at[0], **to_far(0))
+
+    def each_far(body):
+        for distance in range(aux - 1, 0, -1):
+            at = far_layer(distance)
+
+            @pl.when(jnp.logical_and(transit_far == 0, jnp.logical_and(at >= 0, at < aux)))
+            def _():
+                body(distance)
 
     up, down = layer + 1 < aux, layer > 0
 
     barrier = pltpu.get_barrier_semaphore()
     for bit in bits:
         pl.semaphore_signal(barrier, 1, **to_aux(jnp.bitwise_xor(p, bit)))
-    pl.semaphore_signal(barrier, 1, **to_row(next_member))
     pl.semaphore_signal(barrier, 1, **to_row(last_member))
-
-    @pl.when(up)
+    for step in range(1, aux):
+        pl.semaphore_signal(barrier, 1, **to_row(row_of(lax.rem(layer + step, aux), member)))
+
+    @pl.when(main_far > 0)
     def _():
-        pl.semaphore_signal(barrier, 1, **to_row(row_of(layer + 1, member)))
-
-    @pl.when(down)
-    def _():
-        pl.semaphore_signal(barrier, 1, **to_row(row_of(layer - 1, member)))
+        pl.semaphore_signal(
+            barrier, 1, device_id={"aux": partner, "row": row_of(p, member)}, device_id_type=MESH)
+
+    n_far = jnp.where(transit_far == 0, jnp.where(partner < half, aux - 1 - partner, partner), 0)
 
     def own_c(j):
         return pltpu.make_async_copy(
@@ -163,7 +232,7 @@
         own_c(j).start()
     load_b = pltpu.make_async_copy(b_hbm, b, local_b)
     load_b.start()
-    pl.semaphore_wait(barrier, len(bits) + 2 + up.astype(jnp.int32) + down.astype(jnp.int32))
+    pl.semaphore_wait(barrier, len(bits) + aux + n_far)
 
     def loop_from(first, last, body):
         def step(i, carry):
@@ -180,6 +249,19 @@
             for bit in bits:
                 c_aux_piece(j, at_layer, bit).start()
 
+    def first_c():
+        own_c(0).wait()
+        for step in range(1, aux):
+            @pl.when(layer + step < aux)
+            def _():
+                c_direct(layer + step).start()
+
+            @pl.when(layer - step >= 0)
+            def _():
+                c_direct(layer - step).start()
+
+        pass_c(0, layer, True)
+
     def start_c(j, spread=False):
         own_c(j).wait()
 
@@ -193,8 +275,17 @@
 
         pass_c(j, layer, spread)
 
+    def take_first_c():
+        for step in range(1, aux):
+            for at_layer in (layer - step, layer + step):
+                @pl.when(jnp.logical_and(at_layer >= 0, at_layer < aux))
+                def _():
+                    c_line(0, at_layer, 0).wait_recv()
+                    pass_c(0, at_layer, True)
+
     def relay_c(j, spread=False):
         for step in range(1, aux):
+
             @pl.when(layer - step >= 0)
             def _():
                 c_line(j, layer - step, 1).wait_recv()
@@ -218,36 +309,48 @@
     def spread_c(j, spread=False):
         if not spread:
             for bit in bits:
-                c_aux_members(j, member, bit).start()
+                c_aux_members(j, 0, 0, bit).start()
         for step in range(span - 1):
             c_members(j, step).wait_recv()
             if step + 1 < span - 1:
                 for at_layer in range(aux):
                     c_member(j, at_layer, step + 1).start()
             for bit in bits:
-                c_aux_members(j, lax.rem(member + span - 1 - step, span), bit).start()
-
-    def finish_c(j):
+                c_aux_members(j, step + 1, 0, bit).start()
+
+    def finish_c(j, others):
         for k in sorted(range(1, aux), key=lambda k: -(k & -k)):
-            c_aux(j, k ^ (k & -k), k & -k).wait_recv()
+            c_aux_all(j, others, k ^ (k & -k), k & -k).wait_recv()
             for bit in lower(k):
-                c_aux(j, k, bit).start()
-
-    slots = aux * PARTS
-    pieces = slots // 2
+                for step in range(1, span) if others else (0,):
+                    c_aux_members(j, step, k, bit).start()
 
     def transform(j, piece):
+        def block(at_layer, at_member):
+            columns = pl.ds(pl.multiple_of(row_of(at_layer, at_member) * n_rows, n_rows), n_rows)
+            h_acc[...] += jnp.dot(b[:, columns], c[j, at_layer, at_member], preferred_element_type=jnp.float32)
+
+        middle = pieces // 2
+
         @pl.when(piece == 0)
         def _():
-            finish_c(j)
+            finish_c(j, 0)
             h_acc[...] = jnp.zeros_like(h_acc)
 
-        def block(i):
-            h_acc[...] += jnp.dot(
-                b[:, pl.ds(pl.multiple_of(i * n_rows, n_rows), n_rows)], c[j, lax.div(i, span), lax.rem(i, span)],
-                preferred_element_type=jnp.float32)
-
-        loop_from(lax.div(piece * rows_axis, pieces), lax.div((piece + 1) * rows_axis, pieces), block)
+        @pl.when(piece < middle)
+        def _():
+            loop_from(lax.div(piece * aux, middle), lax.div((piece + 1) * aux, middle), lambda i: block(i, member))
+
+        @pl.when(piece == middle)
+        def _():
+            finish_c(j, 1)
+
+        @pl.when(piece >= middle)
+        def _():
+            count = aux * (span - 1)
+            loop_from(
+                lax.div((piece - middle) * count, middle), lax.div((piece - middle + 1) * count, middle),
+                lambda i: block(lax.rem(i, aux), lax.rem(member + 1 + lax.div(i, aux), span)))
 
         @pl.when(piece == pieces - 1)
         def _():
@@ -255,7 +358,13 @@
             for bit in bits:
                 h_aux(j, 0, bit).start()
 
-            @pl.when(j > 0)
+            if not isinstance(j, int) or j >= t_from:
+                @pl.when(jnp.logical_and(j >= t_from, transit_far == 0))
+                def _():
+                    t_member(j).start()
+                    each_far(lambda distance: t_own(j, distance).start())
+
+            @pl.when(j > 1)
             def _():
                 send_rest(j - 1)
 
@@ -264,20 +373,24 @@
             @pl.when(j + 2 < chunks)
             def _():
                 spread_c(j + 2)
+
+    def pass_member(j, i):
+        @pl.when(jnp.logical_not(jnp.logical_and(main_far > 0, by_transit(j, i))))
+        def _():
+            h_member(j, i, 0).start()
+
+    def pass_line(j, i, way):
+        @pl.when(jnp.logical_and(up if way else down, jnp.logical_not(jnp.logical_and(is_far_way(way), by_transit(j, i)))))
+        def _():
+            h_line(j, i, way).start()
 
     def send_h(j, k):
         @pl.when(owner)
         def _():
             def send(i):
-                @pl.when(up)
-                def _():
-                    h_line(j, i, 1).start()
-
-                @pl.when(down)
-                def _():
-                    h_line(j, i, 0).start()
-
-                h_member(j, i, 0).start()
+                pass_line(j, i, 1)
+                pass_line(j, i, 0)
+                pass_member(j, i)
 
             loop_from(k * PARTS, (k + 1) * PARTS, send)
 
@@ -297,25 +410,25 @@
             take_h(j, k)
 
     def relay_h(j, i):
-        @pl.when(layer > p)
-        def _():
-            h_line(j, i, 1).wait_recv()
-
-            @pl.when(up)
-            def _():
-                h_line(j, i, 1).start()
-
-            h_member(j, i, 0).start()
-
-        @pl.when(layer < p)
-        def _():
-            h_line(j, i, 0).wait_recv()
-
-            @pl.when(down)
-            def _():
-                h_line(j, i, 0).start()
-
-            h_member(j, i, 0).start()
+        for way in (1, 0):
+            beyond = layer > p if way else layer < p
+
+            @pl.when(jnp.logical_and(beyond, jnp.logical_not(jnp.logical_and(is_far_way(way), by_transit(j, i)))))
+            def _():
+                h_line(j, i, way).wait_recv()
+                pass_line(j, i, way)
+                pass_member(j, i)
+
+    def relay_t(j):
+        @pl.when(transit_far == 0)
+        def _():
+            t_member(j).wait_recv()
+            each_far(lambda distance: t_other(j, distance).start())
+
+    def take_own(j):
+        @pl.when(jnp.logical_and(main_far > 0, j >= t_from))
+        def _():
+            t_own(jnp.maximum(j, t_from), 0).wait_recv()
 
     tile = min(TILE, n_rows)
     tiles = n_rows // tile
@@ -340,6 +453,8 @@
         def _():
             for half in halves:
                 take_members(j, half)
+            if 1 in halves:
+                take_own(j)
 
         loop_from(lax.div(piece * all_tiles, count), lax.div((piece + 1) * all_tiles, count),
                   lambda n: add_tile(j, n, halves[0] * (aux // 2), (halves[-1] + 1) * (aux // 2)))
@@ -351,12 +466,12 @@
         def other(n):
             add_tile(j, lax.rem(member * tiles + n, all_tiles), aux // 2, aux)
 
+        take_own(j)
         loop(tiles, own)
         take_members(j, 1)
         loop_from(tiles, all_tiles, other)
 
-    start_c(0, True)
-    start_c(1, True)
+    first_c()
 
     def clear(n):
         columns = pl.ds(pl.multiple_of(n * tile, tile), tile)
@@ -364,20 +479,20 @@
 
     loop(span * tiles, clear)
 
-    relay_c(0, True)
+    start_c(1)
+    take_first_c()
     start_c(2)
-    relay_c(1, True)
+    relay_c(1)
     spread_c(0, True)
     start_c(3)
     relay_c(2)
-    spread_c(1, True)
     loop_from(4, chunks, start_c)
-    relay_c(3)
+    spread_c(1)
     load_b.wait()
     loop(pieces // 2, lambda piece: transform(0, piece))
-    loop_from(4, chunks - 1, relay_c)
+    relay_c(3)
     loop_from(pieces // 2, pieces, lambda piece: transform(0, piece))
-    loop_from(max(4, chunks - 1), chunks, relay_c)
+    loop_from(4, chunks, relay_c)
 
     quarter = slots // 4
 
@@ -388,6 +503,15 @@
             chunk = jnp.where(j == 0, jnp.where(i < pieces, 1, 2), jnp.where(early, 2, j + 2))
             piece = jnp.where(
                 j == 0, jnp.where(i < pieces, i, i - 3 * quarter), jnp.where(early, i + quarter, i - quarter))
+
+            @pl.when(jnp.logical_and(j + 1 >= t_from, jnp.logical_and(i == pieces, j + 1 < chunks)))
+            def _():
+                relay_t(j + 1)
+
+            @pl.when(jnp.logical_and(j == 0, i == REST))
+            def _():
+                send_rest(0)
+
             now = jnp.logical_and(jnp.logical_and(piece >= 0, piece < pieces), chunk < chunks)
 
             @pl.when(now)
@@ -402,10 +526,6 @@
             def _():
                 update(j - 1, i - quarter, pieces, (0, 1))
 
-            @pl.when(jnp.logical_and(j == chunks - 1, i >= 3 * quarter))
-            def _():
-                update(j, i - 3 * quarter, quarter, (0,))
-
         loop(slots, slot)
 
         @pl.when(j == max(chunks - 2, 0))
@@ -413,6 +533,7 @@
             send_rest(chunks - 1)
 
     loop(chunks, main)
+    update(chunks - 1, 0, 1, (0,))
     last_update(chunks - 1)
 
     for at in range(aux):
@@ -422,19 +543,44 @@
                 c_line_sent(1, at + 1).wait_send()
             if at > 0:
                 c_line_sent(0, aux - at).wait_send()
+    c_direct_sent().wait_send()
     c_aux_sent().wait_send()
     h_aux_sent().wait_send()
     for step in range(span - 1):
         c_members_sent(step).wait_send()
-        h_member_sent(step).wait_send()
-
-    @pl.when(jnp.logical_and(up, layer >= p))
+        h_member_sent(step, 0, aux).wait_send()
+        fewer = jnp.logical_and(main_far > 0, step == 0)
+
+        @pl.when(fewer)
+        def _():
+            h_member_sent(step, 1, aux - 1).wait_send()
+
+        @pl.when(jnp.logical_not(fewer))
+        def _():
+            h_member_sent(step, 1, aux).wait_send()
+
+    for way, has_next, sends in ((1, up, layer >= p), (0, down, layer <= p)):
+        @pl.when(jnp.logical_and(has_next, sends))
+        def _():
+            h_line_sent(way, 0, aux).wait_send()
+
+            @pl.when(is_far_way(way))
+            def _():
+                h_line_sent(way, 1, aux - 1).wait_send()
+
+            @pl.when(jnp.logical_not(is_far_way(way)))
+            def _():
+                h_line_sent(way, 1, aux).wait_send()
+
+    @pl.when(transit_far == 0)
     def _():
-        h_line_sent(1).wait_send()
-
-    @pl.when(jnp.logical_and(down, layer <= p))
-    def _():
-        h_line_sent(0).wait_send()
+        t_member_sent().wait_send()
+
+    for index in range(aux):
+        @pl.when(jnp.logical_and(transit_far == 0, partner == index))
+        def _():
+            count = aux - 1 - index if index < half else index
+            loop_from(t_from, chunks, lambda j: t_sent(j, count).wait_send())
 
 
 def body(aux, rows_axis, integrals, orbitals):
@@ -455,14 +601,16 @@
             pltpu.VMEM((n_rows, n), integrals.dtype),
             pltpu.VMEM((chunks, aux, span, n_rows, width), orbitals.dtype),
             pltpu.VMEM((1 + span, chunks, n_rows, aux * width), jnp.bfloat16),
+            pltpu.VMEM((chunks - TRANSIT_FROM, n_rows, width), jnp.bfloat16),
             pltpu.VMEM((n_rows, width), jnp.float32),
             dma, dma((chunks,)),
-            dma((2,)), dma((chunks, aux)),
+            dma((3,)), dma((chunks, aux)),
             dma((steps,)), dma((chunks, steps)),
+            dma, dma((chunks, 2, aux)),
             dma, dma((chunks, aux)),
-            dma, dma((chunks, aux)),
-            dma((2,)), dma((chunks, aux * PARTS)),
-            dma((steps,)), dma((chunks, steps, 2)),
+            dma((2, 2)), dma((chunks, aux * PARTS)),
+            dma((steps, 2)), dma((chunks, steps, 2)),
+            dma((chunks - TRANSIT_FROM,)), dma, dma((chunks - TRANSIT_FROM,)),
         ],
         compiler_params=pltpu.CompilerParams(
             collective_id=0, has_side_effects=True, vmem_limit_bytes=54 * 2**20),

time: 199 us -> 193 us (0.970)
  Pallas kernels: 196 us -> 190 us
    pallas_call x1, Pallas kernels: 196 us -> 190 us  [body(): pl.pallas_call(functools.partial(kernel, aux, rows_axis), out_shape=pltpu...]
where the time goes in v5:
time: 193 us
  Pallas kernels  190 us (98%)
  local copies, waits for them, and re-layouts  3.4 us (2%)
    pallas_call x1, Pallas kernels, body(): pl.pallas_call(functools.partial(kernel, aux, rows_axis), out_shape=pltpu...  190 us

profile of v5, /device:TPU:2, one launch (start us, length us, event | category | flops | bytes accessed | tf_op | source)
XLA Modules:
  0.0 193.1 jit_solution(720249747984939411)
XLA Ops:
  0.0 189.7 %shard_map.28 = f32[1024,2048]{1,0:T(8,128)S(1)} custom-call(bf16[1024,8192]{1,0:T(8,128)(2,1)} %bitcast.1, bf16[1024,768]{1,0:T(8,128)(2,1)} %c_hbm.1), custom_call_target="tpu_custom_call" | custom-call | tf_op jit(solution)/shard_map/pallas_call | solution.py:595
  189.7 3.4 %copy.4 = f32[1024,2048]{1,0:T(8,128)} copy(f32[1024,2048]{1,0:T(8,128)S(1)} %shard_map.28) | data formatting | bytes 16777216

commit v6 on v5

--- a/solution.py
+++ b/solution.py
@@ -11,7 +11,9 @@
 CHUNK = 128
 TILE = 256
 PARTS = 4
-REST = 5
+REST = 3
+START = 6
+LATER = 8
 TRANSIT_FROM = 3
 
 
@@ -370,6 +372,9 @@
 
             send_first(j)
 
+            if isinstance(j, int):
+                spread_c(1)
+
             @pl.when(j + 2 < chunks)
             def _():
                 spread_c(j + 2)
@@ -487,7 +492,6 @@
     start_c(3)
     relay_c(2)
     loop_from(4, chunks, start_c)
-    spread_c(1)
     load_b.wait()
     loop(pieces // 2, lambda piece: transform(0, piece))
     relay_c(3)
@@ -499,10 +503,12 @@
     def main(j):
         def slot(i):
             relay_h(j, i)
-            early = jnp.logical_and(j == 1, i < quarter)
-            chunk = jnp.where(j == 0, jnp.where(i < pieces, 1, 2), jnp.where(early, 2, j + 2))
-            piece = jnp.where(
-                j == 0, jnp.where(i < pieces, i, i - 3 * quarter), jnp.where(early, i + quarter, i - quarter))
+            opening = jnp.logical_and(j == 0, i < START + pieces)
+            tail = jnp.logical_and(j == 1, i < START + 2 * pieces - slots)
+            second = jnp.logical_or(tail, jnp.logical_and(j == 0, i >= START + pieces))
+            chunk = jnp.where(opening, 1, jnp.where(second, 2, j + 2))
+            from_zero = j * slots + i - START
+            piece = jnp.where(opening, from_zero, jnp.where(second, from_zero - pieces, i - LATER))
 
             @pl.when(jnp.logical_and(j + 1 >= t_from, jnp.logical_and(i == pieces, j + 1 < chunks)))
             def _():
@@ -518,13 +524,14 @@
             def _():
                 transform(chunk, piece)
 
-            @pl.when(jnp.logical_and(jnp.logical_and(j > 0, j < chunks - 2), i >= 3 * quarter))
-            def _():
-                update(j - 1, i - 3 * quarter, quarter, (0, 1))
-
-            @pl.when(jnp.logical_and(j >= chunks - 2, jnp.logical_and(i >= quarter, i < 3 * quarter)))
-            def _():
-                update(j - 1, i - quarter, pieces, (0, 1))
+            @pl.when(jnp.logical_and(
+                jnp.logical_and(j > 0, j < chunks - 2), jnp.logical_and(i >= quarter, i < 2 * quarter)))
+            def _():
+                update(j - 1, i - quarter, quarter, (0, 1))
+
+            @pl.when(jnp.logical_and(j >= chunks - 2, i >= pieces))
+            def _():
+                update(j - 1, i - pieces, pieces, (0, 1))
 
         loop(slots, slot)
 

time: 193 us -> 192 us (level)
  Pallas kernels: 190 us -> 187 us
    pallas_call x1, Pallas kernels: 190 us -> 187 us  [body(): pl.pallas_call(functools.partial(kernel, aux, rows_axis), out_shape=pltpu...]
where the time goes in v6:
time: 192 us; the launch traced here: 190 us
  Pallas kernels  187 us (97%)
  local copies, waits for them, and re-layouts  3.4 us (2%)
    pallas_call x1, Pallas kernels, body(): pl.pallas_call(functools.partial(kernel, aux, rows_axis), out_shape=pltpu...  187 us

profile of v6, /device:TPU:2, one launch (start us, length us, event | category | flops | bytes accessed | tf_op | source)
XLA Modules:
  0.0 190.3 jit_solution(18426363499774498383)
XLA Ops:
  0.0 186.9 %shard_map.28 = f32[1024,2048]{1,0:T(8,128)S(1)} custom-call(bf16[1024,8192]{1,0:T(8,128)(2,1)} %bitcast.1, bf16[1024,768]{1,0:T(8,128)(2,1)} %c_hbm.1), custom_call_target="tpu_custom_call" | custom-call | tf_op jit(solution)/shard_map/pallas_call | solution.py:602
  186.9 3.4 %copy.4 = f32[1024,2048]{1,0:T(8,128)} copy(f32[1024,2048]{1,0:T(8,128)S(1)} %shard_map.28) | data formatting | bytes 16777216
